TPU v7x, 32 devices: a whole 2x2x4 slice. The times are simulated.
32 devices in a mesh: gx: 4 (over y, x), gy: 2 (over core), gz: 4 (over z).
Axes of the slice: x: 2, y: 2, z: 4, core: 2. Of those that a mesh axis runs over, the one named last changes fastest.
Arguments:
- gradient: bfloat16 [32, 32, 16, 512], P(None, 'gx', 'gy', 'gz'), may hold values from -6 to 6
- noise_draw: bfloat16 [32, 32, 16, 512], P(None, 'gx', 'gy', 'gz'), may hold values from -6 to 6
- current: float32 [32, 32, 16, 512], P(None, 'gx', 'gy', 'gz'), may hold values from -6 to 6
- eigvectors: bfloat16 [32, 16, 512, 512], P('gx', 'gy', 'gz'), may hold values from -0.125 to 0.125
- eigvalues: float32 [512], replicated, may hold values from 0.05 to 50
- reaction: float32 [32, 16, 512], P('gx', 'gy', 'gz'), may hold values from 0.25 to 4
Outputs:
- proposal: float32 [32, 32, 16, 512], P(None, 'gx', 'gy', 'gz')
All inputs are finite; a program needn't handle non-finite values.
Results may differ from a plain program's by a relative error of at most 0.00031.
Values sent between devices are 32-bit elements; how exact they have to be, the bound alone decides.
No kernel may reach another device: no remote copies, remote signals or barrier semaphores. Data moves between devices by JAX's collectives and lax.ppermute only.
A program may use at most 64 MiB of HBM per device.

v0:
```python
import jax
import jax.numpy as jnp
from jax import lax
from jax.sharding import PartitionSpec as P

SWEEPS = 4


def with_halo(block, sides, width):
    for axis, dim in sides:
        count = lax.axis_size(axis)
        forward = [(i, i + 1) for i in range(count - 1)]
        backward = [(target, source) for source, target in forward]
        low = lax.ppermute(
            lax.slice_in_dim(block, block.shape[dim] - width, None, axis=dim), axis, forward
        )
        high = lax.ppermute(lax.slice_in_dim(block, 0, width, axis=dim), axis, backward)
        block = jnp.concatenate([low, block, high], axis=dim)
    return block


def prior_root(source, reaction):
    sweeps = SWEEPS
    diagonal = reaction + 6.0
    field = source / diagonal
    for sweep_index in range(sweeps - 1):
        padded = with_halo(field, (("gx", 1), ("gy", 2), ("gz", 3)), 1)
        total = padded[:, 2:, 1:-1, 1:-1] + padded[:, :-2, 1:-1, 1:-1]
        total = total + padded[:, 1:-1, 2:, 1:-1] + padded[:, 1:-1, :-2, 1:-1]
        total = total + padded[:, 1:-1, 1:-1, 2:] + padded[:, 1:-1, 1:-1, :-2]
        field = (source + total) / diagonal
    return field


def body(gradient, noise_draw, current, eigvectors, eigvalues, reaction):
    chains = gradient.shape[0]
    rank = eigvectors.shape[3]
    cells = reaction.shape[0] * reaction.shape[1] * reaction.shape[2]
    basis = eigvectors.reshape(cells, rank)
    stacked = jnp.concatenate(
        [gradient.reshape(chains, cells), noise_draw.reshape(chains, cells)], 0
    )
    partial_sums = jnp.dot(stacked, basis, preferred_element_type=jnp.float32)
    local_part = -0.5 * gradient.astype(jnp.float32) + 1.0 * noise_draw.astype(jnp.float32)
    sums = lax.psum(partial_sums, ("gx", "gy", "gz"))
    damp = eigvalues / (eigvalues + 1.0)
    root_damp = 1.0 - 1.0 / jnp.sqrt(1.0 + eigvalues)
    coef = (0.5 * damp * sums[:chains] - 1.0 * root_damp * sums[chains:]).astype(jnp.bfloat16)
    corr = lax.dot_general(
        coef, basis, (((1,), (1,)), ((), ())), preferred_element_type=jnp.float32
    )
    field = prior_root(local_part + corr.reshape(current.shape), reaction)
    return current + field


def solution(mesh):
    return jax.shard_map(
        body,
        mesh=mesh,
        in_specs=(
            P(None, "gx", "gy", "gz"),
            P(None, "gx", "gy", "gz"),
            P(None, "gx", "gy", "gz"),
            P("gx", "gy", "gz", None),
            P(),
            P("gx", "gy", "gz"),
        ),
        out_specs=P(None, "gx", "gy", "gz"),
        check_vma=False,
    )
```

profile of v0, /device:TPU:0, one launch (start us, length us, event | category | flops | bytes accessed | tf_op | source)
XLA Modules:
  0.0 262.8 jit_solution(8625238853567087662)
XLA Ops:
  6.5 1.9 copy_bitcast_fusion
  8.4 0.0 copy-start.9
  8.4 0.0 copy-start.10
  8.4 0.0 copy-start
  8.4 0.0 copy-start.1
  8.4 5.7 %fusion.22 = f32[64,512]{1,0:T(8,128)} fusion(bf16[8192,512]{1,0:T(8,128)(2,1)} %bitcast.18, bf16[32,8192]{1,0:T(8,128)(2,1)S(1)} %get-tuple-element.27, bf16[32,8192]{1,0:T(8,128)(2,1)S(1)} %get-tuple-element.28), kind=kOutput, calls=%fused_computation.80 | convolution fusion | flops 538968064 | bytes 9568256 | tf_op jit(solution)/shard_map/dot_general | solution.py:43
  14.1 0.0 all-reduce.2.cloned.1.call-update
  14.2 127.2 %all-reduce.2.cloned.1.call-done = f32[64,512]{1,0:T(8,128)} async-done(((f32[64,512]{1,0:T(8,128)}), f32[64,512]{1,0:T(8,128)}) %all-reduce.2.cloned.1.call-update) | async-done | bytes 131088 | tf_op jit(solution)/shard_map/psum | solution.py:45
  141.5 6.0 %broadcast_divide_fusion = (f32[32,8,8,128]{3,0,2,1:T(8,128)S(1)}, f32[32,8,8,128]{3,0,2,1:T(8,128)S(1)}) fusion(f32[8,8,128]{2,1,0:T(8,128)S(1)} %broadcast_add_fusion, bf16[8,8,128,512]{3,2,1,0:T(8,128)(2,1)} %param.9, f32[64,512]{1,0:T(8,128)} %all-reduce.2.cloned.1.call-done, f32[512]{0:T(512)S(1)} %get-tuple-element.24, f32[512]{0:T(512)S(1)} %get-tuple-element.23, ...), kind=kOutput, calls=%fused_computation.86 | convolution fusion | flops 270073856 | bytes 11702272 | tf_op jit(solution)/shard_map/dot_general | solution.py:49
  147.5 3.4 %collective-permute-start.1 = (f32[32,1,8,128]{3,0,2,1:T(8,128)S(1)}, f32[32,1,8,128]{3,0,2,1:T(8,128)S(1)}, u32[]{:S(2)}, u32[]{:S(2)}) collective-permute-start(f32[32,1,8,128]{3,0,2,1:T(8,128)S(1)} %get-tuple-element.21), channel_id=1, source_target_pairs={{0,8},{8,16},{16,24},{1,9},{9,17},{17,25},{2,10},{10,18},{18,26},{... | collective-permute-start | bytes 393224 | tf_op jit(solution)/shard_map/ppermute | solution.py:14
  150.9 1.3 collective-permute-start
  152.2 1.2 collective-permute-done.1
  153.4 4.7 %collective-permute-done = f32[32,1,8,128]{3,0,2,1:T(8,128)S(1)} collective-permute-done((f32[32,1,8,128]{3,0,2,1:T(8,128)S(1)}, f32[32,1,8,128]{3,0,2,1:T(8,128)S(1)}, u32[]{:S(2)}, u32[]{:S(2)}) %collective-permute-start) | collective-permute-done | bytes 131104 | tf_op jit(solution)/shard_map/ppermute | solution.py:17
  158.1 1.3 collective-permute-start.3
  159.5 1.3 collective-permute-start.2
  160.8 0.0 collective-permute-done.3
  160.8 2.0 collective-permute-done.2
  162.7 0.2 pad_maximum_fusion
  162.9 0.5 copy-done.5
  163.4 2.3 fusion.37
  165.7 2.1 copy.13
  167.7 1.3 collective-permute-start.4
  169.0 2.1 copy.15
  171.1 4.6 %collective-permute-start.5 = (f32[32,10,10,1]{0,3,2,1:T(1,128)S(1)}, f32[32,10,10,1]{0,3,2,1:T(1,128)S(1)}, u32[]{:S(2)}, u32[]{:S(2)}) collective-permute-start(f32[32,10,10,1]{0,3,2,1:T(1,128)S(1)} %copy.15), channel_id=1, source_target_pairs={{0,1},{1,2},{2,3},{4,5},{5,6},{6,7},{8,9},{9,10},{10,11},{12,13},{... | collective-permute-start | bytes 38408 | tf_op jit(solution)/shard_map/ppermute | solution.py:14
  175.7 0.0 collective-permute-done.4
  175.7 1.8 copy.14
  177.5 0.0 collective-permute-done.5
  177.5 1.9 copy.16
  179.4 2.9 %fusion.17 = f32[32,8,8,128]{3,0,2,1:T(8,128)S(1)} fusion(f32[32,8,8,128]{3,0,2,1:T(8,128)S(1)} %get-tuple-element.26, f32[32,10,10,1]{3,0,2,1:T(8,128)} %copy.16, f32[32,10,1,128]{3,0,2,1:T(8,128)} %copy-done.5, f32[32,10,1,128]{3,0,2,1:T(8,128)} %copy-done.3, f32[32,1,8,128]{3,0,2,1:T(8,128)S(1)} %collective-permute-done, ...), kind=kLoop, calls=%fused_computation.58 | loop fusion | flops 6553600 | bytes 3793920 | tf_op jit(solution)/shard_map/div | solution.py:31
  182.3 3.9 %collective-permute-start.7 = (f32[32,1,8,128]{3,0,2,1:T(8,128)S(1)}, f32[32,1,8,128]{3,0,2,1:T(8,128)S(1)}, u32[]{:S(2)}, u32[]{:S(2)}) collective-permute-start(f32[32,1,8,128]{3,0,2,1:T(8,128)S(1)} %get-tuple-element.19), channel_id=1, source_target_pairs={{0,8},{8,16},{16,24},{1,9},{9,17},{17,25},{2,10},{10,18},{18,26},{... | collective-permute-start | bytes 393224 | tf_op jit(solution)/shard_map/ppermute | solution.py:14
  186.3 1.3 collective-permute-start.6
  187.6 1.2 collective-permute-done.7
  188.8 4.4 %collective-permute-done.6 = f32[32,1,8,128]{3,0,2,1:T(8,128)S(1)} collective-permute-done((f32[32,1,8,128]{3,0,2,1:T(8,128)S(1)}, f32[32,1,8,128]{3,0,2,1:T(8,128)S(1)}, u32[]{:S(2)}, u32[]{:S(2)}) %collective-permute-start.6) | collective-permute-done | bytes 131104 | tf_op jit(solution)/shard_map/ppermute | solution.py:17
  193.2 1.3 collective-permute-start.9
  194.5 1.3 collective-permute-start.8
  195.8 2.0 collective-permute-done.8
  197.8 0.2 pad_maximum_fusion.1
  197.9 0.5 copy-done.6
  198.4 2.3 fusion.36
  200.7 2.1 copy.17
  202.7 1.3 collective-permute-start.10
  204.0 2.1 copy.19
  206.1 4.8 %collective-permute-start.11 = (f32[32,10,10,1]{0,3,2,1:T(1,128)S(1)}, f32[32,10,10,1]{0,3,2,1:T(1,128)S(1)}, u32[]{:S(2)}, u32[]{:S(2)}) collective-permute-start(f32[32,10,10,1]{0,3,2,1:T(1,128)S(1)} %copy.19), channel_id=1, source_target_pairs={{0,1},{1,2},{2,3},{4,5},{5,6},{6,7},{8,9},{9,10},{10,11},{12,13},{... | collective-permute-start | bytes 38408 | tf_op jit(solution)/shard_map/ppermute | solution.py:14
  210.9 1.8 copy.18
  212.8 1.9 copy.20
  214.6 2.9 %fusion.10 = f32[32,8,8,128]{3,0,2,1:T(8,128)S(1)} fusion(f32[32,8,8,128]{3,0,2,1:T(8,128)S(1)} %get-tuple-element.26, f32[32,10,10,1]{3,0,2,1:T(8,128)} %copy.20, f32[32,10,1,128]{3,0,2,1:T(8,128)} %copy-done.6, f32[32,10,1,128]{3,0,2,1:T(8,128)} %copy-done.4, f32[32,1,8,128]{3,0,2,1:T(8,128)S(1)} %collective-permute-done.6, ...), kind=kLoop, calls=%fused_computation.33 | loop fusion | flops 6553600 | bytes 3793920 | tf_op jit(solution)/shard_map/div | solution.py:31
  217.5 3.4 %collective-permute-start.13 = (f32[32,1,8,128]{3,0,2,1:T(8,128)S(1)}, f32[32,1,8,128]{3,0,2,1:T(8,128)S(1)}, u32[]{:S(2)}, u32[]{:S(2)}) collective-permute-start(f32[32,1,8,128]{3,0,2,1:T(8,128)S(1)} %get-tuple-element.17), channel_id=1, source_target_pairs={{0,8},{8,16},{16,24},{1,9},{9,17},{17,25},{2,10},{10,18},{18,26},{... | collective-permute-start | bytes 393224 | tf_op jit(solution)/shard_map/ppermute | solution.py:14
  220.9 1.3 collective-permute-start.12
  222.2 1.5 collective-permute-done.13
  223.7 4.1 %collective-permute-done.12 = f32[32,1,8,128]{3,0,2,1:T(8,128)S(1)} collective-permute-done((f32[32,1,8,128]{3,0,2,1:T(8,128)S(1)}, f32[32,1,8,128]{3,0,2,1:T(8,128)S(1)}, u32[]{:S(2)}, u32[]{:S(2)}) %collective-permute-start.12) | collective-permute-done | bytes 131104 | tf_op jit(solution)/shard_map/ppermute | solution.py:17
  227.8 1.3 collective-permute-start.15
  229.1 1.3 collective-permute-start.14
  230.5 2.0 collective-permute-done.14
  232.4 0.2 pad_maximum_fusion.2
  232.6 0.5 copy-done.8
  233.1 2.2 fusion.35
  235.3 2.1 copy.21
  237.4 1.3 collective-permute-start.16
  238.7 2.7 %copy.23 = f32[32,10,10,1]{0,3,2,1:T(1,128)} copy(f32[32,10,10,1]{3,0,2,1:T(8,128)} %get-tuple-element.6) | data formatting | bytes 25600 | tf_op jit(solution)/shard_map/slice | solution.py:15
  241.4 5.5 %collective-permute-start.17 = (f32[32,10,10,1]{0,3,2,1:T(1,128)}, f32[32,10,10,1]{0,3,2,1:T(1,128)}, u32[]{:S(2)}, u32[]{:S(2)}) collective-permute-start(f32[32,10,10,1]{0,3,2,1:T(1,128)} %copy.23), channel_id=1, source_target_pairs={{0,1},{1,2},{2,3},{4,5},{5,6},{6,7},{8,9},{9,10},{10,11},{12,13},{... | collective-permute-start | bytes 38408 | tf_op jit(solution)/shard_map/ppermute | solution.py:14
  246.9 1.9 copy.22
  248.8 2.6 %copy.24 = f32[32,10,10,1]{3,0,2,1:T(8,128)} copy(f32[32,10,10,1]{0,3,2,1:T(1,128)} %collective-permute-done.17) | data formatting | bytes 25600 | tf_op jit(solution)/shard_map/ppermute | solution.py:14
  251.4 3.0 %fusion.3 = f32[32,8,8,128]{3,0,2,1:T(8,128)S(1)} fusion(f32[32,8,8,128]{3,0,2,1:T(8,128)S(1)} %get-tuple-element.26, f32[32,10,10,1]{3,0,2,1:T(8,128)} %copy.24, f32[32,10,1,128]{3,0,2,1:T(8,128)} %copy-done.8, f32[32,10,1,128]{3,0,2,1:T(8,128)} %copy-done.7, f32[32,1,8,128]{3,0,2,1:T(8,128)S(1)} %collective-permute-done.12, ...), kind=kLoop, calls=%fused_computation.8 | loop fusion | flops 6815744 | bytes 4842496 | tf_op jit(solution)/shard_map/add | solution.py:53
  254.4 1.6 copy.26
  (30 shorter events, 0.2 us)
Async XLA Ops:
  6.5 134.9 %all-reduce.2.cloned.1.call-start = ((), (), s32[]{:S(2)}) async-start(), calls=%async_computation | async-start | bytes 262144 | tf_op jit(solution)/shard_map/psum | solution.py:45
  8.4 5.8 %copy-start.9 = (f32[8,8,128]{2,1,0:T(8,128)S(1)}, f32[8,8,128]{2,1,0:T(8,128)}, u32[]{:S(2)}) copy-start(f32[8,8,128]{2,1,0:T(8,128)} %param.11) | copy-start | bytes 98308
  8.4 5.8 %copy-start.10 = (f32[512]{0:T(512)S(1)}, f32[512]{0:T(512)}, u32[]{:S(2)}) copy-start(f32[512]{0:T(512)} %param.10) | copy-start | bytes 6148
  8.4 133.0 %copy-start = (bf16[32,8,8,128]{3,2,1,0:T(8,128)(2,1)S(1)}, bf16[32,8,8,128]{3,2,1,0:T(8,128)(2,1)}, u32[]{:S(2)}) copy-start(bf16[32,8,8,128]{3,2,1,0:T(8,128)(2,1)} %param.7) | copy-start | bytes 1572868
  8.4 133.0 %copy-start.1 = (bf16[32,8,8,128]{3,2,1,0:T(8,128)(2,1)S(1)}, bf16[32,8,8,128]{3,2,1,0:T(8,128)(2,1)}, u32[]{:S(2)}) copy-start(bf16[32,8,8,128]{3,2,1,0:T(8,128)(2,1)} %param.6) | copy-start | bytes 1572868
  147.5 5.9 %collective-permute-start.1 = (f32[32,1,8,128]{3,0,2,1:T(8,128)S(1)}, f32[32,1,8,128]{3,0,2,1:T(8,128)S(1)}, u32[]{:S(2)}, u32[]{:S(2)}) collective-permute-start(f32[32,1,8,128]{3,0,2,1:T(8,128)S(1)} %get-tuple-element.21), channel_id=1, source_target_pairs={{0,8},{8,16},{16,24},{1,9},{9,17},{17,25},{2,10},{10,18},{18,26},{... | collective-permute-start | bytes 393224 | tf_op jit(solution)/shard_map/ppermute | solution.py:14
  150.9 7.2 %collective-permute-start = (f32[32,1,8,128]{3,0,2,1:T(8,128)S(1)}, f32[32,1,8,128]{3,0,2,1:T(8,128)S(1)}, u32[]{:S(2)}, u32[]{:S(2)}) collective-permute-start(f32[32,1,8,128]{3,0,2,1:T(8,128)S(1)} %get-tuple-element.22), channel_id=1, source_target_pairs={{8,0},{16,8},{24,16},{9,1},{17,9},{25,17},{10,2},{18,10},{26,18},{... | collective-permute-start | bytes 393224 | tf_op jit(solution)/shard_map/ppermute | solution.py:17
  158.1 2.6 collective-permute-start.3
  159.5 3.3 %collective-permute-start.2 = (f32[32,10,1,128]{3,0,2,1:T(8,128)S(1)}, f32[32,10,1,128]{3,0,2,1:T(8,128)S(1)}, u32[]{:S(2)}, u32[]{:S(2)}) collective-permute-start(f32[32,10,1,128]{3,0,2,1:T(8,128)S(1)} %get-tuple-element.16), channel_id=1, source_target_pairs={{4,0},{5,1},{6,2},{7,3},{12,8},{13,9},{14,10},{15,11},{20,16},{21,... | collective-permute-start | bytes 491528 | tf_op jit(solution)/shard_map/ppermute | solution.py:17
  160.8 2.2 copy-start.3
  162.7 0.7 copy-start.5
  167.7 7.9 %collective-permute-start.4 = (f32[32,10,10,1]{0,3,2,1:T(1,128)S(1)}, f32[32,10,10,1]{0,3,2,1:T(1,128)S(1)}, u32[]{:S(2)}, u32[]{:S(2)}) collective-permute-start(f32[32,10,10,1]{0,3,2,1:T(1,128)S(1)} %copy.13), channel_id=1, source_target_pairs={{1,0},{2,1},{3,2},{5,4},{6,5},{7,6},{9,8},{10,9},{11,10},{13,12},{... | collective-permute-start | bytes 38408 | tf_op jit(solution)/shard_map/ppermute | solution.py:17
  171.1 6.4 %collective-permute-start.5 = (f32[32,10,10,1]{0,3,2,1:T(1,128)S(1)}, f32[32,10,10,1]{0,3,2,1:T(1,128)S(1)}, u32[]{:S(2)}, u32[]{:S(2)}) collective-permute-start(f32[32,10,10,1]{0,3,2,1:T(1,128)S(1)} %copy.15), channel_id=1, source_target_pairs={{0,1},{1,2},{2,3},{4,5},{5,6},{6,7},{8,9},{9,10},{10,11},{12,13},{... | collective-permute-start | bytes 38408 | tf_op jit(solution)/shard_map/ppermute | solution.py:14
  182.3 6.4 %collective-permute-start.7 = (f32[32,1,8,128]{3,0,2,1:T(8,128)S(1)}, f32[32,1,8,128]{3,0,2,1:T(8,128)S(1)}, u32[]{:S(2)}, u32[]{:S(2)}) collective-permute-start(f32[32,1,8,128]{3,0,2,1:T(8,128)S(1)} %get-tuple-element.19), channel_id=1, source_target_pairs={{0,8},{8,16},{16,24},{1,9},{9,17},{17,25},{2,10},{10,18},{18,26},{... | collective-permute-start | bytes 393224 | tf_op jit(solution)/shard_map/ppermute | solution.py:14
  186.3 6.9 %collective-permute-start.6 = (f32[32,1,8,128]{3,0,2,1:T(8,128)S(1)}, f32[32,1,8,128]{3,0,2,1:T(8,128)S(1)}, u32[]{:S(2)}, u32[]{:S(2)}) collective-permute-start(f32[32,1,8,128]{3,0,2,1:T(8,128)S(1)} %get-tuple-element.20), channel_id=1, source_target_pairs={{8,0},{16,8},{24,16},{9,1},{17,9},{25,17},{10,2},{18,10},{26,18},{... | collective-permute-start | bytes 393224 | tf_op jit(solution)/shard_map/ppermute | solution.py:17
  193.2 2.6 collective-permute-start.9
  194.5 3.3 %collective-permute-start.8 = (f32[32,10,1,128]{3,0,2,1:T(8,128)S(1)}, f32[32,10,1,128]{3,0,2,1:T(8,128)S(1)}, u32[]{:S(2)}, u32[]{:S(2)}) collective-permute-start(f32[32,10,1,128]{3,0,2,1:T(8,128)S(1)} %get-tuple-element.14), channel_id=1, source_target_pairs={{4,0},{5,1},{6,2},{7,3},{12,8},{13,9},{14,10},{15,11},{20,16},{21,... | collective-permute-start | bytes 491528 | tf_op jit(solution)/shard_map/ppermute | solution.py:17
  195.8 2.2 copy-start.4
  197.8 0.7 copy-start.6
  202.7 8.2 %collective-permute-start.10 = (f32[32,10,10,1]{0,3,2,1:T(1,128)S(1)}, f32[32,10,10,1]{0,3,2,1:T(1,128)S(1)}, u32[]{:S(2)}, u32[]{:S(2)}) collective-permute-start(f32[32,10,10,1]{0,3,2,1:T(1,128)S(1)} %copy.17), channel_id=1, source_target_pairs={{1,0},{2,1},{3,2},{5,4},{6,5},{7,6},{9,8},{10,9},{11,10},{13,12},{... | collective-permute-start | bytes 38408 | tf_op jit(solution)/shard_map/ppermute | solution.py:17
  206.1 6.6 %collective-permute-start.11 = (f32[32,10,10,1]{0,3,2,1:T(1,128)S(1)}, f32[32,10,10,1]{0,3,2,1:T(1,128)S(1)}, u32[]{:S(2)}, u32[]{:S(2)}) collective-permute-start(f32[32,10,10,1]{0,3,2,1:T(1,128)S(1)} %copy.19), channel_id=1, source_target_pairs={{0,1},{1,2},{2,3},{4,5},{5,6},{6,7},{8,9},{9,10},{10,11},{12,13},{... | collective-permute-start | bytes 38408 | tf_op jit(solution)/shard_map/ppermute | solution.py:14
  217.5 6.1 %collective-permute-start.13 = (f32[32,1,8,128]{3,0,2,1:T(8,128)S(1)}, f32[32,1,8,128]{3,0,2,1:T(8,128)S(1)}, u32[]{:S(2)}, u32[]{:S(2)}) collective-permute-start(f32[32,1,8,128]{3,0,2,1:T(8,128)S(1)} %get-tuple-element.17), channel_id=1, source_target_pairs={{0,8},{8,16},{16,24},{1,9},{9,17},{17,25},{2,10},{10,18},{18,26},{... | collective-permute-start | bytes 393224 | tf_op jit(solution)/shard_map/ppermute | solution.py:14
  220.9 6.9 %collective-permute-start.12 = (f32[32,1,8,128]{3,0,2,1:T(8,128)S(1)}, f32[32,1,8,128]{3,0,2,1:T(8,128)S(1)}, u32[]{:S(2)}, u32[]{:S(2)}) collective-permute-start(f32[32,1,8,128]{3,0,2,1:T(8,128)S(1)} %get-tuple-element.18), channel_id=1, source_target_pairs={{8,0},{16,8},{24,16},{9,1},{17,9},{25,17},{10,2},{18,10},{26,18},{... | collective-permute-start | bytes 393224 | tf_op jit(solution)/shard_map/ppermute | solution.py:17
  227.8 2.6 collective-permute-start.15
  229.1 3.3 %collective-permute-start.14 = (f32[32,10,1,128]{3,0,2,1:T(8,128)S(1)}, f32[32,10,1,128]{3,0,2,1:T(8,128)S(1)}, u32[]{:S(2)}, u32[]{:S(2)}) collective-permute-start(f32[32,10,1,128]{3,0,2,1:T(8,128)S(1)} %get-tuple-element.12), channel_id=1, source_target_pairs={{4,0},{5,1},{6,2},{7,3},{12,8},{13,9},{14,10},{15,11},{20,16},{21,... | collective-permute-start | bytes 491528 | tf_op jit(solution)/shard_map/ppermute | solution.py:17
  230.4 2.2 copy-start.7
  232.4 0.7 copy-start.8
  237.4 9.5 %collective-permute-start.16 = (f32[32,10,10,1]{0,3,2,1:T(1,128)S(1)}, f32[32,10,10,1]{0,3,2,1:T(1,128)S(1)}, u32[]{:S(2)}, u32[]{:S(2)}) collective-permute-start(f32[32,10,10,1]{0,3,2,1:T(1,128)S(1)} %copy.21), channel_id=1, source_target_pairs={{1,0},{2,1},{3,2},{5,4},{6,5},{7,6},{9,8},{10,9},{11,10},{13,12},{... | collective-permute-start | bytes 38408 | tf_op jit(solution)/shard_map/ppermute | solution.py:17
  241.4 10.0 %copy-start.2 = (f32[32,8,8,128]{3,2,1,0:T(8,128)S(1)}, f32[32,8,8,128]{3,2,1,0:T(8,128)}, u32[]{:S(2)}) copy-start(f32[32,8,8,128]{3,2,1,0:T(8,128)} %param.8) | copy-start | bytes 3145732
  241.4 7.4 %collective-permute-start.17 = (f32[32,10,10,1]{0,3,2,1:T(1,128)}, f32[32,10,10,1]{0,3,2,1:T(1,128)}, u32[]{:S(2)}, u32[]{:S(2)}) collective-permute-start(f32[32,10,10,1]{0,3,2,1:T(1,128)} %copy.23), channel_id=1, source_target_pairs={{0,1},{1,2},{2,3},{4,5},{5,6},{6,7},{8,9},{9,10},{10,11},{12,13},{... | collective-permute-start | bytes 38408 | tf_op jit(solution)/shard_map/ppermute | solution.py:14
Sparse Core Ops, SparseCore 0:
  14.3 127.1 all-reduce.1
where the time goes:
time: 264 us; the launch traced here: 263 us
  waiting for transfers between devices  150 us (57%)
  starting transfers between devices  41.1 us (16%)
  local copies, waits for them, and re-layouts  36.7 us (14%)
  between operations  13.8 us (5%)
  matrix products  11.7 us (4%)
  other arithmetic  9.37 us (4%)
    psum x1, waiting for transfers between devices, body(): sums = lax.psum(partial_sums, ('gx', 'gy', 'gz'))  127 us
    ppermute x9, starting transfers between devices, with_halo(): lax.ppermute(lax.slice_in_dim(block, block.shape[dim] - width, None, axis...  29.4 us
    ppermute x9, waiting for transfers between devices, with_halo(): lax.ppermute(lax.slice_in_dim(block, 0, width, axis=dim), axis, backward)  19.1 us
    slice x6, local copies, waits for them, and re-layouts, with_halo(): lax.slice_in_dim(block, 0, width, axis=dim)  13 us
    ppermute x9, starting transfers between devices, with_halo(): lax.ppermute(lax.slice_in_dim(block, 0, width, axis=dim), axis, backward)  11.6 us
    slice x6, local copies, waits for them, and re-layouts, with_halo(): lax.slice_in_dim(block, block.shape[dim] - width, None, axis=dim)  6.9 us
    ppermute x3, local copies, waits for them, and re-layouts, with_halo(): lax.ppermute(lax.slice_in_dim(block, block.shape[dim] - width, None, axis...  6.34 us
    dot_general x1, matrix products, body(): lax.dot_general(coef, basis, (((1,), (1,)), ((), ())), preferred_element_...  6.04 us
  transfers between devices with their start and end apart: 19, of which 10 were waited for; matrix products, arithmetic and copies ran while one was open for 5% of the time, Pallas kernels for 0%

commit v1 on v0

v1 whole, which is shorter than its diff:
```python
import jax
import jax.numpy as jnp
from jax import lax
from jax.experimental import pallas as pl
from jax.experimental.pallas import tpu as pltpu
from jax.sharding import PartitionSpec as P

SWEEPS = 4


def reduce_over(value, axis):
    count = lax.axis_size(axis)
    if count & (count - 1):
        return lax.psum(value, axis)
    step = 1
    while step < count:
        value = value + lax.ppermute(value, axis, [(i, i ^ step) for i in range(count)])
        step *= 2
    return value


def lines(axis):
    count = lax.axis_size(axis)
    forward = [(i, i + 1) for i in range(count - 1)]
    return forward, [(target, source) for source, target in forward]


def put_column(packed, lane, where, column):
    return jnp.where(lane == where, column, packed)


def expand_kernel(total_ref, basis_ref, local_ref, inverse_ref, source_ref, field_ref, low_ref, high_ref):
    x = pl.program_id(0)
    _, rows, cells, rank = basis_ref.shape
    chains = total_ref.shape[0]
    coef = total_ref[...].astype(jnp.bfloat16)
    basis = basis_ref[...].reshape(rows * cells, rank)
    corr = lax.dot_general(coef, basis, (((1,), (1,)), ((), ())), preferred_element_type=jnp.float32)
    lane = lax.broadcasted_iota(jnp.int32, low_ref.shape, 1)
    low, high = low_ref[...], high_ref[...]
    for y in range(rows):
        source = local_ref[0, y] + corr[:, y * cells:(y + 1) * cells]
        field = source * inverse_ref[0, y:y + 1, :]
        source_ref[0, y] = source
        field_ref[0, y] = field
        low = put_column(low, lane, x * rows + y, field[:, :1])
        high = put_column(high, lane, x * rows + y, field[:, cells - 1:])
    low_ref[...] = low
    high_ref[...] = high


def expand(total, basis, local, inverse):
    planes, rows, cells, rank = basis.shape
    chains = total.shape[0]
    whole = jax.ShapeDtypeStruct((planes, rows, chains, cells), jnp.float32)
    face = jax.ShapeDtypeStruct((chains, planes * rows), jnp.float32)
    return pl.pallas_call(
        expand_kernel,
        grid=(planes,),
        in_specs=[
            pl.BlockSpec((chains, rank), lambda x: (0, 0)),
            pl.BlockSpec((1, rows, cells, rank), lambda x: (x, 0, 0, 0)),
            pl.BlockSpec((1, rows, chains, cells), lambda x: (x, 0, 0, 0)),
            pl.BlockSpec((1, rows, cells), lambda x: (x, 0, 0)),
        ],
        out_specs=[
            pl.BlockSpec((1, rows, chains, cells), lambda x: (x, 0, 0, 0)),
            pl.BlockSpec((1, rows, chains, cells), lambda x: (x, 0, 0, 0)),
            pl.BlockSpec((chains, planes * rows), lambda x: (0, 0)),
            pl.BlockSpec((chains, planes * rows), lambda x: (0, 0)),
        ],
        out_shape=[whole, whole, face, face],
        name="expand",
        compiler_params=pltpu.CompilerParams(vmem_limit_bytes=24 * 2**20),
    )(total, basis, local, inverse)


def new_field(refs, x, y, lane):
    mask_ref, field_ref, source_ref, inverse_ref, xlow_ref, xhigh_ref, ylow_ref, yhigh_ref, zlow_ref, zhigh_ref = refs
    planes, rows, chains, cells = field_ref.shape
    here = field_ref[x, y]
    place = x * rows + y
    value = source_ref[x, y]
    value = value + (field_ref[x + 1, y] if x + 1 < planes else xhigh_ref[0, y])
    value = value + (field_ref[x - 1, y] if x > 0 else xlow_ref[0, y])
    value = value + (field_ref[x, y + 1] if y + 1 < rows else yhigh_ref[x, 0] * mask_ref[1])
    value = value + (field_ref[x, y - 1] if y > 0 else ylow_ref[x, 0] * mask_ref[0])
    value = value + jnp.where(lane == 0, zlow_ref[:, place:place + 1], pltpu.roll(here, 1, 1))
    value = value + jnp.where(lane == cells - 1, zhigh_ref[:, place:place + 1], pltpu.roll(here, cells - 1, 1))
    return value * inverse_ref[x, y:y + 1, :]


def sweep_kernel(*refs):
    *inputs, out_ref, low_ref, high_ref = refs
    planes, rows, chains, cells = out_ref.shape
    lane = lax.broadcasted_iota(jnp.int32, (chains, cells), 1)
    face_lane = lax.broadcasted_iota(jnp.int32, low_ref.shape, 1)
    low = jnp.zeros(low_ref.shape, jnp.float32)
    high = jnp.zeros(high_ref.shape, jnp.float32)
    for x in range(planes):
        for y in range(rows):
            value = new_field(inputs, x, y, lane)
            out_ref[x, y] = value
            low = put_column(low, face_lane, x * rows + y, value[:, :1])
            high = put_column(high, face_lane, x * rows + y, value[:, cells - 1:])
    low_ref[...] = low
    high_ref[...] = high


def last_kernel(*refs):
    *inputs, current_ref, out_ref = refs
    chains, planes, rows, cells = out_ref.shape
    lane = lax.broadcasted_iota(jnp.int32, (chains, cells), 1)
    for x in range(planes):
        plane = jnp.stack([new_field(inputs, x, y, lane) for y in range(rows)])
        out_ref[:, x] = current_ref[:, x] + jnp.swapaxes(plane, 0, 1)


def specs(count):
    return [pl.BlockSpec(memory_space=pltpu.SMEM)] + [pl.BlockSpec(memory_space=pltpu.VMEM)] * count


def near(*arrays):
    return [pltpu.with_memory_space_constraint(a, pltpu.VMEM) for a in arrays]


def halo(field, low, high):
    forward, backward = lines("gx")
    xlow = lax.ppermute(field[-1:], "gx", forward)
    xhigh = lax.ppermute(field[:1], "gx", backward)
    forward, backward = lines("gz")
    zlow = lax.ppermute(high, "gz", forward)
    zhigh = lax.ppermute(low, "gz", backward)
    if lax.axis_size("gy") == 2:
        send = jnp.where(lax.axis_index("gy") == 0, field[:, -1:], field[:, :1])
        ylow = yhigh = lax.ppermute(send, "gy", [(0, 1), (1, 0)])
    else:
        forward, backward = lines("gy")
        ylow = lax.ppermute(field[:, -1:], "gy", forward)
        yhigh = lax.ppermute(field[:, :1], "gy", backward)
    return xlow, xhigh, ylow, yhigh, zlow, zhigh


def body(gradient, noise_draw, current, eigvectors, eigvalues, reaction):
    chains = gradient.shape[0]
    rank = eigvectors.shape[3]
    cells = reaction.size
    basis = eigvectors.reshape(cells, rank)
    stacked = jnp.concatenate(
        [gradient.reshape(chains, cells), noise_draw.reshape(chains, cells)], 0
    )
    partial_sums = jnp.dot(stacked, basis, preferred_element_type=jnp.float32)
    damp = eigvalues / (eigvalues + 1.0)
    root_damp = 1.0 - 1.0 / jnp.sqrt(1.0 + eigvalues)
    total = 0.5 * damp * partial_sums[:chains] - 1.0 * root_damp * partial_sums[chains:]
    for axis in ("gy", "gz", "gx"):
        total = reduce_over(total, axis)
    local = -0.5 * gradient.astype(jnp.float32) + 1.0 * noise_draw.astype(jnp.float32)
    local = jnp.transpose(local, (1, 2, 0, 3))
    inverse = 1.0 / (reaction + 6.0)
    last = lax.axis_size("gy") - 1
    place = lax.axis_index("gy")
    mask = jnp.where(jnp.arange(2) == 0, place > 0, place < last).astype(jnp.float32)

    source, field, low, high = expand(total, eigvectors, local, inverse)
    for _ in range(SWEEPS - 2):
        field, low, high = pl.pallas_call(
            sweep_kernel,
            in_specs=specs(9),
            out_specs=[pl.BlockSpec(memory_space=pltpu.VMEM)] * 3,
            out_shape=[pltpu.VMEM(a.shape, jnp.float32) for a in (field, low, high)],
            name="sweep",
            compiler_params=pltpu.CompilerParams(vmem_limit_bytes=16 * 2**20),
        )(mask, *near(field, source, inverse, *halo(field, low, high)))
    return pl.pallas_call(
        last_kernel,
        in_specs=specs(10),
        out_specs=pl.BlockSpec(memory_space=pltpu.VMEM),
        out_shape=jax.ShapeDtypeStruct(current.shape, jnp.float32),
        name="last_sweep",
        compiler_params=pltpu.CompilerParams(vmem_limit_bytes=16 * 2**20),
    )(mask, *near(field, source, inverse, *halo(field, low, high), current))


def solution(mesh):
    return jax.shard_map(
        body,
        mesh=mesh,
        in_specs=(
            P(None, "gx", "gy", "gz"),
            P(None, "gx", "gy", "gz"),
            P(None, "gx", "gy", "gz"),
            P("gx", "gy", "gz", None),
            P(),
            P("gx", "gy", "gz"),
        ),
        out_specs=P(None, "gx", "gy", "gz"),
        check_vma=False,
    )
```

time: 264 us -> 102 us (0.39)
  waiting for transfers between devices: 150 us -> 23 us
  local copies, waits for them, and re-layouts: 36.7 us -> 6.02 us
  Pallas kernels: 0 us -> 21.2 us
  between operations: 13.8 us -> 0.28 us
  other arithmetic: 9.37 us -> 2.12 us
  matrix products: 11.7 us -> 5.02 us
  starting transfers between devices: 41.1 us -> 44.2 us
    psum x1 -> x0, waiting for transfers between devices: 127 us -> none  [body(): sums = lax.psum(partial_sums, ('gx', 'gy', 'gz'))]
    pallas_call x0 -> x4, Pallas kernels: none -> 21.2 us  [the longest x2 13.9 us: body(): pl.pallas_call(sweep_kernel, in_specs=specs(9), out_specs=[pl.BlockSpec(m...]
    slice x12 -> x3, local copies, waits for them, and re-layouts: 19.9 us -> 0.75 us  [halo(): xhigh = lax.ppermute(field[:1], 'gx', backward)]
    ppermute x6 -> x0, local copies, waits for them, and re-layouts: 11.9 us -> none  [the longest x3 6.34 us: with_halo(): lax.ppermute(lax.slice_in_dim(block, block.shape[dim] - width, None, axis...]
    dot_general x1 -> x0, matrix products: 6.04 us -> none  [body(): lax.dot_general(coef, basis, (((1,), (1,)), ((), ())), preferred_element_...]
    div x2 -> x1, other arithmetic: 5.8 us -> 0.01 us  [body(): inverse = 1.0 / (reaction + 6.0)]
    ppermute x18 -> x20, starting transfers between devices: 41.1 us -> 44.2 us  [the longest x3 15 us: halo(): xlow = lax.ppermute(field[-1:], 'gx', forward)]
    add x2 -> x5, other arithmetic: 2.99 us -> 0.06 us  [reduce_over(): value + lax.ppermute(value, axis, [(i, i ^ step) for i in range(count)])]
  transfers between devices with their start and end apart: 19 -> 20, of which waited for: 10 -> 11; matrix products, arithmetic and copies ran while one was open for 5% -> 1% of each run, Pallas kernels for 0% -> 0%
where the time goes in v1:
time: 102 us
  starting transfers between devices  44.2 us (43%)
  waiting for transfers between devices  23 us (23%)
  Pallas kernels  21.2 us (21%)
  local copies, waits for them, and re-layouts  6.02 us (6%)
  matrix products  5.02 us (5%)
  other arithmetic  2.12 us (2%)
    ppermute x3, starting transfers between devices, halo(): xlow = lax.ppermute(field[-1:], 'gx', forward)  15 us
    pallas_call x2, Pallas kernels, body(): pl.pallas_call(sweep_kernel, in_specs=specs(9), out_specs=[pl.BlockSpec(m...  13.9 us
    ppermute x3, waiting for transfers between devices, halo(): zhigh = lax.ppermute(low, 'gz', backward)  12.6 us
    ppermute x3, starting transfers between devices, halo(): zlow = lax.ppermute(high, 'gz', forward)  11.3 us
    ppermute x5, starting transfers between devices, reduce_over(): lax.ppermute(value, axis, [(i, i ^ step) for i in range(count)])  10.1 us
    ppermute x5, waiting for transfers between devices, reduce_over(): lax.ppermute(value, axis, [(i, i ^ step) for i in range(count)])  10 us
    dot_general x1, matrix products, body(): partial_sums = jnp.dot(stacked, basis, preferred_element_type=jnp.float32)  5.02 us
    pallas_call x1, Pallas kernels, expand(): pl.pallas_call(expand_kernel, grid=(planes,), in_specs=[pl.BlockSpec((cha...  4.24 us
  transfers between devices with their start and end apart: 20, of which 11 were waited for; matrix products, arithmetic and copies ran while one was open for 1% of the time, Pallas kernels for 0%

profile of v1, /device:TPU:0, one launch (start us, length us, event | category | flops | bytes accessed | tf_op | source)
XLA Modules:
  0.0 101.8 jit_solution(2117456632118186623)
XLA Ops:
  0.0 0.7 fusion.5
  0.7 1.9 %copy_bitcast_fusion = (bf16[32,8192]{1,0:T(8,128)(2,1)S(1)}, bf16[32,8192]{1,0:T(8,128)(2,1)S(1)}) fusion(bf16[4,8,64,128]{3,2,1,0:T(8,128)(2,1)} %bitcast.13, bf16[4,8,64,128]{3,2,1,0:T(8,128)(2,1)} %bitcast.14), kind=kLoop, calls=%fused_computation.5 | loop fusion | bytes 2097152 | tf_op jit(solution)/shard_map/reshape | solution.py:150
  2.6 0.0 copy-start.2
  2.6 0.0 copy-start.3
  2.6 0.0 copy-start.4
  2.6 5.0 %fusion = f32[64,512]{1,0:T(8,128)S(1)} fusion(bf16[8192,512]{1,0:T(8,128)(2,1)} %bitcast.12, bf16[32,8192]{1,0:T(8,128)(2,1)S(1)} %get-tuple-element.33, bf16[32,8192]{1,0:T(8,128)(2,1)S(1)} %get-tuple-element.34), kind=kOutput, calls=%fused_computation | convolution fusion | flops 538968064 | bytes 9568256 | tf_op jit(solution)/shard_map/dot_general | solution.py:152
  7.6 0.6 collective-permute-start
  8.2 0.9 collective-permute-done
  9.1 3.0 %collective-permute-start.1 = (f32[32,512]{1,0:T(8,128)S(1)}, f32[32,512]{1,0:T(8,128)S(1)}, u32[]{:S(2)}, u32[]{:S(2)}) collective-permute-start(f32[32,512]{1,0:T(8,128)S(1)} %fusion.12), channel_id=1, source_target_pairs={{0,1},{1,0},{2,3},{3,2},{4,5},{5,4},{6,7},{7,6},{8,9},{9,8},{10,11... | collective-permute-start | bytes 196616 | tf_op jit(solution)/shard_map/ppermute | solution.py:17
  12.1 2.4 %collective-permute-done.1 = f32[32,512]{1,0:T(8,128)S(1)} collective-permute-done((f32[32,512]{1,0:T(8,128)S(1)}, f32[32,512]{1,0:T(8,128)S(1)}, u32[]{:S(2)}, u32[]{:S(2)}) %collective-permute-start.1) | collective-permute-done | bytes 65568 | tf_op jit(solution)/shard_map/ppermute | solution.py:17
  14.5 2.9 %collective-permute-start.2 = (f32[32,512]{1,0:T(8,128)S(1)}, f32[32,512]{1,0:T(8,128)S(1)}, u32[]{:S(2)}, u32[]{:S(2)}) collective-permute-start(f32[32,512]{1,0:T(8,128)S(1)} %add.30), channel_id=1, source_target_pairs={{0,2},{1,3},{2,0},{3,1},{4,6},{5,7},{6,4},{7,5},{8,10},{9,11},{10,... | collective-permute-start | bytes 196616 | tf_op jit(solution)/shard_map/ppermute | solution.py:17
  17.5 2.3 %collective-permute-done.2 = f32[32,512]{1,0:T(8,128)S(1)} collective-permute-done((f32[32,512]{1,0:T(8,128)S(1)}, f32[32,512]{1,0:T(8,128)S(1)}, u32[]{:S(2)}, u32[]{:S(2)}) %collective-permute-start.2) | collective-permute-done | bytes 65568 | tf_op jit(solution)/shard_map/ppermute | solution.py:17
  19.8 1.8 %collective-permute-start.3 = (f32[32,512]{1,0:T(8,128)S(1)}, f32[32,512]{1,0:T(8,128)S(1)}, u32[]{:S(2)}, u32[]{:S(2)}) collective-permute-start(f32[32,512]{1,0:T(8,128)S(1)} %add.31), channel_id=1, source_target_pairs={{0,8},{8,0},{16,24},{24,16},{1,9},{9,1},{17,25},{25,17},{2,10},{10... | collective-permute-start | bytes 196616 | tf_op jit(solution)/shard_map/ppermute | solution.py:17
  21.6 0.0 copy-done.2
  21.6 0.0 copy-done.3
  21.6 0.6 add_bitcast_fusion.local_ref
  22.2 1.9 %collective-permute-done.3 = f32[32,512]{1,0:T(8,128)S(1)} collective-permute-done((f32[32,512]{1,0:T(8,128)S(1)}, f32[32,512]{1,0:T(8,128)S(1)}, u32[]{:S(2)}, u32[]{:S(2)}) %collective-permute-start.3) | collective-permute-done | bytes 65568 | tf_op jit(solution)/shard_map/ppermute | solution.py:17
  24.1 1.8 %collective-permute-start.4 = (f32[32,512]{1,0:T(8,128)S(1)}, f32[32,512]{1,0:T(8,128)S(1)}, u32[]{:S(2)}, u32[]{:S(2)}) collective-permute-start(f32[32,512]{1,0:T(8,128)S(1)} %add.32), channel_id=1, source_target_pairs={{0,16},{8,24},{16,0},{24,8},{1,17},{9,25},{17,1},{25,9},{2,18},{10... | collective-permute-start | bytes 196616 | tf_op jit(solution)/shard_map/ppermute | solution.py:17
  26.0 0.0 copy-done.4
  26.0 2.5 %collective-permute-done.4 = f32[32,512]{1,0:T(8,128)S(1)} collective-permute-done((f32[32,512]{1,0:T(8,128)S(1)}, f32[32,512]{1,0:T(8,128)S(1)}, u32[]{:S(2)}, u32[]{:S(2)}) %collective-permute-start.4) | collective-permute-done | bytes 65568 | tf_op jit(solution)/shard_map/ppermute | solution.py:17
  28.5 0.0 copy-start
  28.5 3.4 %copy-done = bf16[8,8,128,512]{3,2,1,0:T(8,128)(2,1)S(1)} copy-done((bf16[8,8,128,512]{3,2,1,0:T(8,128)(2,1)S(1)}, bf16[8,8,128,512]{3,2,1,0:T(8,128)(2,1)}, u32[]{:S(2)}) %copy-start) | copy-done | bytes 8388632
  31.9 4.2 %expand.1 = (f32[8,8,32,128]{3,2,1,0:T(8,128)S(1)}, f32[8,8,32,128]{3,2,1,0:T(8,128)S(1)}, f32[32,64]{1,0:T(8,128)S(1)}, f32[32,64]{1,0:T(8,128)S(1)}) custom-call(f32[32,512]{1,0:T(8,128)S(1)} %add.33.total_ref, bf16[8,8,128,512]{3,2,1,0:T(8,128)(2,1)S(1)} %copy-done, f32[8,8,32,128]{3,2,1,0:T(8,128)S(1)} %add_bitcast_fusion.local_ref, ...), custom_call_target="tpu_custom_call" | custom-call | tf_op jit(solution)/shard_map/expand/pallas_call | solution.py:57
  36.1 0.0 copy-start.1
  36.1 0.7 fusion.10
  36.9 0.7 slice_select_fusion.2
  37.5 0.0 collective-permute-start.7
  37.5 1.3 %collective-permute-start.6 = (f32[1,8,32,128]{3,2,1,0:T(8,128)}, f32[1,8,32,128]{3,2,1,0:T(8,128)S(1)}, u32[]{:S(2)}, u32[]{:S(2)}) collective-permute-start(f32[1,8,32,128]{3,2,1,0:T(8,128)} %get-tuple-element.29), channel_id=1, source_target_pairs={{8,0},{16,8},{24,16},{9,1},{17,9},{25,17},{10,2},{18,10},{26,18},{... | collective-permute-start | bytes 393224 | tf_op jit(solution)/shard_map/ppermute | solution.py:130
  38.8 5.2 %collective-permute-start.5 = (f32[1,8,32,128]{3,2,1,0:T(8,128)}, f32[1,8,32,128]{3,2,1,0:T(8,128)}, u32[]{:S(2)}, u32[]{:S(2)}) collective-permute-start(f32[1,8,32,128]{3,2,1,0:T(8,128)} %get-tuple-element.30), channel_id=1, source_target_pairs={{0,8},{8,16},{16,24},{1,9},{9,17},{17,25},{2,10},{10,18},{18,26},{... | collective-permute-start | bytes 393224 | tf_op jit(solution)/shard_map/ppermute | solution.py:129
  44.0 3.7 %collective-permute-start.8 = (f32[32,64]{1,0:T(8,128)S(1)}, f32[32,64]{1,0:T(8,128)S(1)}, u32[]{:S(2)}, u32[]{:S(2)}) collective-permute-start(f32[32,64]{1,0:T(8,128)S(1)} %get-tuple-element.17), channel_id=1, source_target_pairs={{0,1},{1,2},{2,3},{4,5},{5,6},{6,7},{8,9},{9,10},{10,11},{12,13},{... | collective-permute-start | bytes 24584 | tf_op jit(solution)/shard_map/ppermute | solution.py:132
  47.8 1.3 %collective-permute-start.9 = (f32[32,64]{1,0:T(8,128)S(1)}, f32[32,64]{1,0:T(8,128)S(1)}, u32[]{:S(2)}, u32[]{:S(2)}) collective-permute-start(f32[32,64]{1,0:T(8,128)S(1)} %get-tuple-element.18), channel_id=1, source_target_pairs={{1,0},{2,1},{3,2},{5,4},{6,5},{7,6},{9,8},{10,9},{11,10},{13,12},{... | collective-permute-start | bytes 24584 | tf_op jit(solution)/shard_map/ppermute | solution.py:133
  49.1 0.1 collective-permute-done.8.refs_8_
  49.2 4.2 %collective-permute-done.9.refs_9_ = f32[32,64]{1,0:T(8,128)S(1)} collective-permute-done((f32[32,64]{1,0:T(8,128)S(1)}, f32[32,64]{1,0:T(8,128)S(1)}, u32[]{:S(2)}, u32[]{:S(2)}) %collective-permute-start.9) | collective-permute-done | bytes 8224 | tf_op jit(solution)/shard_map/ppermute | solution.py:133
  53.4 0.0 collective-permute-done.7.refs_6_.refs_7_
  53.4 0.0 collective-permute-done.6.refs_5_
  53.4 0.0 collective-permute-done.5.refs_4_
  53.4 7.1 %sweep.2 = (f32[8,8,32,128]{3,2,1,0:T(8,128)S(1)}, f32[32,64]{1,0:T(8,128)S(1)}, f32[32,64]{1,0:T(8,128)S(1)}) custom-call(f32[2]{0:T(128)S(1)} %select_convert_fusion.refs_0_, f32[8,8,32,128]{3,2,1,0:T(8,128)S(1)} %get-tuple-element.15.refs_1_, f32[8,8,32,128]{3,2,1,0:T(8,128)S(1)} %get-tuple-element.16.refs_2_, ...), custom_call_target="tpu_custom_call" | custom-call | tf_op jit(solution)/shard_map/sweep/pallas_call | solution.py:167
  60.6 0.1 collective-permute-start.12
  60.7 1.3 %collective-permute-start.11 = (f32[1,8,32,128]{3,2,1,0:T(8,128)S(1)}, f32[1,8,32,128]{3,2,1,0:T(8,128)S(1)}, u32[]{:S(2)}, u32[]{:S(2)}) collective-permute-start(f32[1,8,32,128]{3,2,1,0:T(8,128)S(1)} %get-tuple-element.27), channel_id=1, source_target_pairs={{8,0},{16,8},{24,16},{9,1},{17,9},{25,17},{10,2},{18,10},{26,18},{... | collective-permute-start | bytes 393224 | tf_op jit(solution)/shard_map/ppermute | solution.py:130
  62.0 4.6 %collective-permute-start.10 = (f32[1,8,32,128]{3,2,1,0:T(8,128)S(1)}, f32[1,8,32,128]{3,2,1,0:T(8,128)S(1)}, u32[]{:S(2)}, u32[]{:S(2)}) collective-permute-start(f32[1,8,32,128]{3,2,1,0:T(8,128)S(1)} %get-tuple-element.28), channel_id=1, source_target_pairs={{0,8},{8,16},{16,24},{1,9},{9,17},{17,25},{2,10},{10,18},{18,26},{... | collective-permute-start | bytes 393224 | tf_op jit(solution)/shard_map/ppermute | solution.py:129
  66.6 3.6 %collective-permute-start.13 = (f32[32,64]{1,0:T(8,128)S(1)}, f32[32,64]{1,0:T(8,128)S(1)}, u32[]{:S(2)}, u32[]{:S(2)}) collective-permute-start(f32[32,64]{1,0:T(8,128)S(1)} %get-tuple-element.20), channel_id=1, source_target_pairs={{0,1},{1,2},{2,3},{4,5},{5,6},{6,7},{8,9},{9,10},{10,11},{12,13},{... | collective-permute-start | bytes 24584 | tf_op jit(solution)/shard_map/ppermute | solution.py:132
  70.2 1.3 %collective-permute-start.14 = (f32[32,64]{1,0:T(8,128)S(1)}, f32[32,64]{1,0:T(8,128)S(1)}, u32[]{:S(2)}, u32[]{:S(2)}) collective-permute-start(f32[32,64]{1,0:T(8,128)S(1)} %get-tuple-element.21), channel_id=1, source_target_pairs={{1,0},{2,1},{3,2},{5,4},{6,5},{7,6},{9,8},{10,9},{11,10},{13,12},{... | collective-permute-start | bytes 24584 | tf_op jit(solution)/shard_map/ppermute | solution.py:133
  71.5 0.1 collective-permute-done.13.refs_8_
  71.6 4.2 %collective-permute-done.14.refs_9_ = f32[32,64]{1,0:T(8,128)S(1)} collective-permute-done((f32[32,64]{1,0:T(8,128)S(1)}, f32[32,64]{1,0:T(8,128)S(1)}, u32[]{:S(2)}, u32[]{:S(2)}) %collective-permute-start.14) | collective-permute-done | bytes 8224 | tf_op jit(solution)/shard_map/ppermute | solution.py:133
  75.8 0.0 collective-permute-done.12.refs_6_.refs_7_
  75.8 0.0 collective-permute-done.11.refs_5_
  75.8 0.0 collective-permute-done.10.refs_4_
  75.8 6.8 %sweep.3 = (f32[8,8,32,128]{3,2,1,0:T(8,128)S(1)}, f32[32,64]{1,0:T(8,128)S(1)}, f32[32,64]{1,0:T(8,128)S(1)}) custom-call(f32[2]{0:T(128)S(1)} %select_convert_fusion.refs_0_, f32[8,8,32,128]{3,2,1,0:T(8,128)S(1)} %get-tuple-element.19.refs_1_, f32[8,8,32,128]{3,2,1,0:T(8,128)S(1)} %get-tuple-element.16.refs_2_, ...), custom_call_target="tpu_custom_call" | custom-call | tf_op jit(solution)/shard_map/sweep/pallas_call | solution.py:167
  82.7 0.1 collective-permute-start.17
  82.8 1.3 %collective-permute-start.16 = (f32[1,8,32,128]{3,2,1,0:T(8,128)S(1)}, f32[1,8,32,128]{3,2,1,0:T(8,128)S(1)}, u32[]{:S(2)}, u32[]{:S(2)}) collective-permute-start(f32[1,8,32,128]{3,2,1,0:T(8,128)S(1)} %get-tuple-element.25), channel_id=1, source_target_pairs={{8,0},{16,8},{24,16},{9,1},{17,9},{25,17},{10,2},{18,10},{26,18},{... | collective-permute-start | bytes 393224 | tf_op jit(solution)/shard_map/ppermute | solution.py:130
  84.1 5.2 %collective-permute-start.15 = (f32[1,8,32,128]{3,2,1,0:T(8,128)S(1)}, f32[1,8,32,128]{3,2,1,0:T(8,128)S(1)}, u32[]{:S(2)}, u32[]{:S(2)}) collective-permute-start(f32[1,8,32,128]{3,2,1,0:T(8,128)S(1)} %get-tuple-element.26), channel_id=1, source_target_pairs={{0,8},{8,16},{16,24},{1,9},{9,17},{17,25},{2,10},{10,18},{18,26},{... | collective-permute-start | bytes 393224 | tf_op jit(solution)/shard_map/ppermute | solution.py:129
  89.3 3.9 %collective-permute-start.18 = (f32[32,64]{1,0:T(8,128)S(1)}, f32[32,64]{1,0:T(8,128)S(1)}, u32[]{:S(2)}, u32[]{:S(2)}) collective-permute-start(f32[32,64]{1,0:T(8,128)S(1)} %get-tuple-element.23), channel_id=1, source_target_pairs={{0,1},{1,2},{2,3},{4,5},{5,6},{6,7},{8,9},{9,10},{10,11},{12,13},{... | collective-permute-start | bytes 24584 | tf_op jit(solution)/shard_map/ppermute | solution.py:132
  93.2 1.3 %collective-permute-start.19 = (f32[32,64]{1,0:T(8,128)S(1)}, f32[32,64]{1,0:T(8,128)S(1)}, u32[]{:S(2)}, u32[]{:S(2)}) collective-permute-start(f32[32,64]{1,0:T(8,128)S(1)} %get-tuple-element.24), channel_id=1, source_target_pairs={{1,0},{2,1},{3,2},{5,4},{6,5},{7,6},{9,8},{10,9},{11,10},{13,12},{... | collective-permute-start | bytes 24584 | tf_op jit(solution)/shard_map/ppermute | solution.py:133
  94.5 0.1 collective-permute-done.18.refs_8_
  94.6 4.2 %collective-permute-done.19.refs_9_ = f32[32,64]{1,0:T(8,128)S(1)} collective-permute-done((f32[32,64]{1,0:T(8,128)S(1)}, f32[32,64]{1,0:T(8,128)S(1)}, u32[]{:S(2)}, u32[]{:S(2)}) %collective-permute-start.19) | collective-permute-done | bytes 8224 | tf_op jit(solution)/shard_map/ppermute | solution.py:133
  98.8 0.0 collective-permute-done.17.refs_6_.refs_7_
  98.8 0.0 collective-permute-done.16.refs_5_
  98.8 0.0 collective-permute-done.15.refs_4_
  98.8 0.0 copy-done.1
  98.8 3.0 %last_sweep.1 = f32[32,8,8,128]{3,2,1,0:T(8,128)} custom-call(f32[2]{0:T(128)S(1)} %select_convert_fusion.refs_0_, f32[8,8,32,128]{3,2,1,0:T(8,128)S(1)} %get-tuple-element.22.refs_1_, f32[8,8,32,128]{3,2,1,0:T(8,128)S(1)} %get-tuple-element.16.refs_2_, f32[8,8,128]{2,1,0:T(8,128)S(1)} %add_divide_fusion.inverse_ref.refs_3_, ...), custom_call_target="tpu_custom_call" | custom-call | tf_op jit(solution)/shard_map/last_sweep/pallas_call | solution.py:175
  (12 shorter events, 0.2 us)
Async XLA Ops:
  2.6 19.1 %copy-start.2 = (bf16[32,8,8,128]{3,2,1,0:T(8,128)(2,1)S(1)}, bf16[32,8,8,128]{3,2,1,0:T(8,128)(2,1)}, u32[]{:S(2)}) copy-start(bf16[32,8,8,128]{3,2,1,0:T(8,128)(2,1)} %param.7) | copy-start | bytes 1572868
  2.6 19.0 %copy-start.3 = (bf16[32,8,8,128]{3,2,1,0:T(8,128)(2,1)S(1)}, bf16[32,8,8,128]{3,2,1,0:T(8,128)(2,1)}, u32[]{:S(2)}) copy-start(bf16[32,8,8,128]{3,2,1,0:T(8,128)(2,1)} %param.6) | copy-start | bytes 1572868
  2.6 23.4 %copy-start.4 = (f32[8,8,128]{2,1,0:T(8,128)S(1)}, f32[8,8,128]{2,1,0:T(8,128)}, u32[]{:S(2)}) copy-start(f32[8,8,128]{2,1,0:T(8,128)} %param.11) | copy-start | bytes 98308
  7.6 1.5 %collective-permute-start = (f32[32,512]{1,0:T(8,128)S(1)}, f32[32,512]{1,0:T(8,128)S(1)}, u32[]{:S(2)}, u32[]{:S(2)}) collective-permute-start(f32[32,512]{1,0:T(8,128)S(1)} %fusion.4), channel_id=1, source_target_pairs={{0,4},{4,0},{1,5},{5,1},{2,6},{6,2},{3,7},{7,3},{8,12},{12,8},{9,1... | collective-permute-start | bytes 196616 | tf_op jit(solution)/shard_map/ppermute | solution.py:17
  9.1 5.4 %collective-permute-start.1 = (f32[32,512]{1,0:T(8,128)S(1)}, f32[32,512]{1,0:T(8,128)S(1)}, u32[]{:S(2)}, u32[]{:S(2)}) collective-permute-start(f32[32,512]{1,0:T(8,128)S(1)} %fusion.12), channel_id=1, source_target_pairs={{0,1},{1,0},{2,3},{3,2},{4,5},{5,4},{6,7},{7,6},{8,9},{9,8},{10,11... | collective-permute-start | bytes 196616 | tf_op jit(solution)/shard_map/ppermute | solution.py:17
  14.5 5.3 %collective-permute-start.2 = (f32[32,512]{1,0:T(8,128)S(1)}, f32[32,512]{1,0:T(8,128)S(1)}, u32[]{:S(2)}, u32[]{:S(2)}) collective-permute-start(f32[32,512]{1,0:T(8,128)S(1)} %add.30), channel_id=1, source_target_pairs={{0,2},{1,3},{2,0},{3,1},{4,6},{5,7},{6,4},{7,5},{8,10},{9,11},{10,... | collective-permute-start | bytes 196616 | tf_op jit(solution)/shard_map/ppermute | solution.py:17
  19.8 4.3 %collective-permute-start.3 = (f32[32,512]{1,0:T(8,128)S(1)}, f32[32,512]{1,0:T(8,128)S(1)}, u32[]{:S(2)}, u32[]{:S(2)}) collective-permute-start(f32[32,512]{1,0:T(8,128)S(1)} %add.31), channel_id=1, source_target_pairs={{0,8},{8,0},{16,24},{24,16},{1,9},{9,1},{17,25},{25,17},{2,10},{10... | collective-permute-start | bytes 196616 | tf_op jit(solution)/shard_map/ppermute | solution.py:17
  24.1 4.3 %collective-permute-start.4 = (f32[32,512]{1,0:T(8,128)S(1)}, f32[32,512]{1,0:T(8,128)S(1)}, u32[]{:S(2)}, u32[]{:S(2)}) collective-permute-start(f32[32,512]{1,0:T(8,128)S(1)} %add.32), channel_id=1, source_target_pairs={{0,16},{8,24},{16,0},{24,8},{1,17},{9,25},{17,1},{25,9},{2,18},{10... | collective-permute-start | bytes 196616 | tf_op jit(solution)/shard_map/ppermute | solution.py:17
  28.5 3.4 %copy-start = (bf16[8,8,128,512]{3,2,1,0:T(8,128)(2,1)S(1)}, bf16[8,8,128,512]{3,2,1,0:T(8,128)(2,1)}, u32[]{:S(2)}) copy-start(bf16[8,8,128,512]{3,2,1,0:T(8,128)(2,1)} %basis_ref.1) | copy-start | bytes 25165828
  36.1 62.7 %copy-start.1 = (f32[32,8,8,128]{3,2,1,0:T(8,128)S(1)}, f32[32,8,8,128]{3,2,1,0:T(8,128)}, u32[]{:S(2)}) copy-start(f32[32,8,8,128]{3,2,1,0:T(8,128)} %refs_10_.1) | copy-start | bytes 3145732
  37.5 15.9 %collective-permute-start.7 = (f32[8,1,32,128]{3,2,1,0:T(8,128)}, f32[8,1,32,128]{3,2,1,0:T(8,128)S(1)}, u32[]{:S(2)}, u32[]{:S(2)}) collective-permute-start(f32[8,1,32,128]{3,2,1,0:T(8,128)} %slice_select_fusion.2), channel_id=1, source_target_pairs={{0,4},{4,0},{1,5},{5,1},{2,6},{6,2},{3,7},{7,3},{8,12},{12,8},{9,1... | collective-permute-start | bytes 393224 | tf_op jit(solution)/shard_map/ppermute | solution.py:136
  37.5 15.9 %collective-permute-start.6 = (f32[1,8,32,128]{3,2,1,0:T(8,128)}, f32[1,8,32,128]{3,2,1,0:T(8,128)S(1)}, u32[]{:S(2)}, u32[]{:S(2)}) collective-permute-start(f32[1,8,32,128]{3,2,1,0:T(8,128)} %get-tuple-element.29), channel_id=1, source_target_pairs={{8,0},{16,8},{24,16},{9,1},{17,9},{25,17},{10,2},{18,10},{26,18},{... | collective-permute-start | bytes 393224 | tf_op jit(solution)/shard_map/ppermute | solution.py:130
  38.8 14.6 %collective-permute-start.5 = (f32[1,8,32,128]{3,2,1,0:T(8,128)}, f32[1,8,32,128]{3,2,1,0:T(8,128)}, u32[]{:S(2)}, u32[]{:S(2)}) collective-permute-start(f32[1,8,32,128]{3,2,1,0:T(8,128)} %get-tuple-element.30), channel_id=1, source_target_pairs={{0,8},{8,16},{16,24},{1,9},{9,17},{17,25},{2,10},{10,18},{18,26},{... | collective-permute-start | bytes 393224 | tf_op jit(solution)/shard_map/ppermute | solution.py:129
  44.0 5.1 %collective-permute-start.8 = (f32[32,64]{1,0:T(8,128)S(1)}, f32[32,64]{1,0:T(8,128)S(1)}, u32[]{:S(2)}, u32[]{:S(2)}) collective-permute-start(f32[32,64]{1,0:T(8,128)S(1)} %get-tuple-element.17), channel_id=1, source_target_pairs={{0,1},{1,2},{2,3},{4,5},{5,6},{6,7},{8,9},{9,10},{10,11},{12,13},{... | collective-permute-start | bytes 24584 | tf_op jit(solution)/shard_map/ppermute | solution.py:132
  47.8 5.6 %collective-permute-start.9 = (f32[32,64]{1,0:T(8,128)S(1)}, f32[32,64]{1,0:T(8,128)S(1)}, u32[]{:S(2)}, u32[]{:S(2)}) collective-permute-start(f32[32,64]{1,0:T(8,128)S(1)} %get-tuple-element.18), channel_id=1, source_target_pairs={{1,0},{2,1},{3,2},{5,4},{6,5},{7,6},{9,8},{10,9},{11,10},{13,12},{... | collective-permute-start | bytes 24584 | tf_op jit(solution)/shard_map/ppermute | solution.py:133
  60.6 15.2 %collective-permute-start.12 = (f32[8,1,32,128]{3,2,1,0:T(8,128)S(1)}, f32[8,1,32,128]{3,2,1,0:T(8,128)S(1)}, u32[]{:S(2)}, u32[]{:S(2)}) collective-permute-start(f32[8,1,32,128]{3,2,1,0:T(8,128)S(1)} %slice_select_fusion.1), channel_id=1, source_target_pairs={{0,4},{4,0},{1,5},{5,1},{2,6},{6,2},{3,7},{7,3},{8,12},{12,8},{9,1... | collective-permute-start | bytes 393224 | tf_op jit(solution)/shard_map/ppermute | solution.py:136
  60.7 15.1 %collective-permute-start.11 = (f32[1,8,32,128]{3,2,1,0:T(8,128)S(1)}, f32[1,8,32,128]{3,2,1,0:T(8,128)S(1)}, u32[]{:S(2)}, u32[]{:S(2)}) collective-permute-start(f32[1,8,32,128]{3,2,1,0:T(8,128)S(1)} %get-tuple-element.27), channel_id=1, source_target_pairs={{8,0},{16,8},{24,16},{9,1},{17,9},{25,17},{10,2},{18,10},{26,18},{... | collective-permute-start | bytes 393224 | tf_op jit(solution)/shard_map/ppermute | solution.py:130
  62.0 13.8 %collective-permute-start.10 = (f32[1,8,32,128]{3,2,1,0:T(8,128)S(1)}, f32[1,8,32,128]{3,2,1,0:T(8,128)S(1)}, u32[]{:S(2)}, u32[]{:S(2)}) collective-permute-start(f32[1,8,32,128]{3,2,1,0:T(8,128)S(1)} %get-tuple-element.28), channel_id=1, source_target_pairs={{0,8},{8,16},{16,24},{1,9},{9,17},{17,25},{2,10},{10,18},{18,26},{... | collective-permute-start | bytes 393224 | tf_op jit(solution)/shard_map/ppermute | solution.py:129
  66.6 5.1 %collective-permute-start.13 = (f32[32,64]{1,0:T(8,128)S(1)}, f32[32,64]{1,0:T(8,128)S(1)}, u32[]{:S(2)}, u32[]{:S(2)}) collective-permute-start(f32[32,64]{1,0:T(8,128)S(1)} %get-tuple-element.20), channel_id=1, source_target_pairs={{0,1},{1,2},{2,3},{4,5},{5,6},{6,7},{8,9},{9,10},{10,11},{12,13},{... | collective-permute-start | bytes 24584 | tf_op jit(solution)/shard_map/ppermute | solution.py:132
  70.2 5.6 %collective-permute-start.14 = (f32[32,64]{1,0:T(8,128)S(1)}, f32[32,64]{1,0:T(8,128)S(1)}, u32[]{:S(2)}, u32[]{:S(2)}) collective-permute-start(f32[32,64]{1,0:T(8,128)S(1)} %get-tuple-element.21), channel_id=1, source_target_pairs={{1,0},{2,1},{3,2},{5,4},{6,5},{7,6},{9,8},{10,9},{11,10},{13,12},{... | collective-permute-start | bytes 24584 | tf_op jit(solution)/shard_map/ppermute | solution.py:133
  82.7 16.1 %collective-permute-start.17 = (f32[8,1,32,128]{3,2,1,0:T(8,128)S(1)}, f32[8,1,32,128]{3,2,1,0:T(8,128)S(1)}, u32[]{:S(2)}, u32[]{:S(2)}) collective-permute-start(f32[8,1,32,128]{3,2,1,0:T(8,128)S(1)} %slice_select_fusion), channel_id=1, source_target_pairs={{0,4},{4,0},{1,5},{5,1},{2,6},{6,2},{3,7},{7,3},{8,12},{12,8},{9,1... | collective-permute-start | bytes 393224 | tf_op jit(solution)/shard_map/ppermute | solution.py:136
  82.8 16.1 %collective-permute-start.16 = (f32[1,8,32,128]{3,2,1,0:T(8,128)S(1)}, f32[1,8,32,128]{3,2,1,0:T(8,128)S(1)}, u32[]{:S(2)}, u32[]{:S(2)}) collective-permute-start(f32[1,8,32,128]{3,2,1,0:T(8,128)S(1)} %get-tuple-element.25), channel_id=1, source_target_pairs={{8,0},{16,8},{24,16},{9,1},{17,9},{25,17},{10,2},{18,10},{26,18},{... | collective-permute-start | bytes 393224 | tf_op jit(solution)/shard_map/ppermute | solution.py:130
  84.1 14.8 %collective-permute-start.15 = (f32[1,8,32,128]{3,2,1,0:T(8,128)S(1)}, f32[1,8,32,128]{3,2,1,0:T(8,128)S(1)}, u32[]{:S(2)}, u32[]{:S(2)}) collective-permute-start(f32[1,8,32,128]{3,2,1,0:T(8,128)S(1)} %get-tuple-element.26), channel_id=1, source_target_pairs={{0,8},{8,16},{16,24},{1,9},{9,17},{17,25},{2,10},{10,18},{18,26},{... | collective-permute-start | bytes 393224 | tf_op jit(solution)/shard_map/ppermute | solution.py:129
  89.3 5.4 %collective-permute-start.18 = (f32[32,64]{1,0:T(8,128)S(1)}, f32[32,64]{1,0:T(8,128)S(1)}, u32[]{:S(2)}, u32[]{:S(2)}) collective-permute-start(f32[32,64]{1,0:T(8,128)S(1)} %get-tuple-element.23), channel_id=1, source_target_pairs={{0,1},{1,2},{2,3},{4,5},{5,6},{6,7},{8,9},{9,10},{10,11},{12,13},{... | collective-permute-start | bytes 24584 | tf_op jit(solution)/shard_map/ppermute | solution.py:132
  93.2 5.6 %collective-permute-start.19 = (f32[32,64]{1,0:T(8,128)S(1)}, f32[32,64]{1,0:T(8,128)S(1)}, u32[]{:S(2)}, u32[]{:S(2)}) collective-permute-start(f32[32,64]{1,0:T(8,128)S(1)} %get-tuple-element.24), channel_id=1, source_target_pairs={{1,0},{2,1},{3,2},{5,4},{6,5},{7,6},{9,8},{10,9},{11,10},{13,12},{... | collective-permute-start | bytes 24584 | tf_op jit(solution)/shard_map/ppermute | solution.py:133

commit v2 on v0

v2 whole, which is shorter than its diff:
```python
import jax
import jax.numpy as jnp
from jax import lax
from jax.experimental import pallas as pl
from jax.experimental.pallas import tpu as pltpu
from jax.sharding import PartitionSpec as P

SWEEPS = 4


def reduce_over(value, axis):
    count = lax.axis_size(axis)
    if count & (count - 1):
        return lax.psum(value, axis)
    step = 1
    while step < count:
        value = value + lax.ppermute(value, axis, [(i, i ^ step) for i in range(count)])
        step *= 2
    return value


def lines(axis):
    count = lax.axis_size(axis)
    forward = [(i, i + 1) for i in range(count - 1)]
    return forward, [(target, source) for source, target in forward]


def put_faces(packed, field, plane):
    rows, chains, cells = field.shape
    slots = cells // 2
    pair = lax.broadcasted_iota(jnp.int32, (chains, cells), 1) // 2
    for y in range(rows):
        group, slot = divmod(plane * rows + y, slots)
        turned = pltpu.roll(field[y], (2 * slot + 1) % cells, 1)
        packed[group] = jnp.where(pair == slot, turned, packed[group])


def blank_faces(faces_ref):
    return [jnp.zeros(faces_ref.shape[1:], jnp.float32) for _ in range(faces_ref.shape[0])]


def slab_copies(basis_hbm, basis_ref, sems):
    return [
        pltpu.make_async_copy(basis_hbm.at[x], basis_ref.at[x], sems.at[x])
        for x in range(basis_ref.shape[0])
    ]


def project_kernel(
    gradient_hbm, noise_hbm, basis_hbm, eigvalues_ref, mixed_ref,
    gradient_ref, noise_ref, basis_ref, data_sems, basis_sems,
):
    planes, rows, cells, rank = basis_ref.shape
    chains = mixed_ref.shape[0]
    data = [
        pltpu.make_async_copy(gradient_hbm, gradient_ref, data_sems.at[0]),
        pltpu.make_async_copy(noise_hbm, noise_ref, data_sems.at[1]),
    ]
    slabs = slab_copies(basis_hbm, basis_ref, basis_sems)
    for copy in data + slabs:
        copy.start()
    for copy in data:
        copy.wait()
    sums = jnp.zeros((2 * chains, rank), jnp.float32)
    for x in range(planes):
        gradient = jnp.swapaxes(gradient_ref[:, x].astype(jnp.float32), 0, 1)
        noise = jnp.swapaxes(noise_ref[:, x].astype(jnp.float32), 0, 1)
        stacked = jnp.concatenate([gradient, noise], 1).astype(jnp.bfloat16)
        stacked = jnp.concatenate([stacked[y] for y in range(rows)], 1)
        slabs[x].wait()
        slab = basis_ref[x].reshape(rows * cells, rank)
        sums = sums + jnp.dot(stacked, slab, preferred_element_type=jnp.float32)
    values = eigvalues_ref[...]
    damp = values / (values + 1.0)
    root_damp = 1.0 - 1.0 / jnp.sqrt(1.0 + values)
    mixed_ref[...] = 0.5 * damp * sums[:chains] - 1.0 * root_damp * sums[chains:]


def project(gradient, noise_draw, eigvectors, eigvalues):
    planes, rows, cells, rank = eigvectors.shape
    chains = gradient.shape[0]
    outside = pl.BlockSpec(memory_space=pltpu.HBM)
    inside = pl.BlockSpec(memory_space=pltpu.VMEM)
    return pl.pallas_call(
        project_kernel,
        in_specs=[outside, outside, outside, inside],
        out_specs=inside,
        out_shape=pltpu.VMEM((chains, rank), jnp.float32),
        scratch_shapes=[
            pltpu.VMEM(gradient.shape, gradient.dtype),
            pltpu.VMEM(noise_draw.shape, noise_draw.dtype),
            pltpu.VMEM(eigvectors.shape, eigvectors.dtype),
            pltpu.SemaphoreType.DMA((2,)),
            pltpu.SemaphoreType.DMA((planes,)),
        ],
        compiler_params=pltpu.CompilerParams(vmem_limit_bytes=60 * 2**20),
        name="project",
    )(gradient, noise_draw, eigvectors, eigvalues.reshape(1, rank))


def expand_kernel(
    total_ref, basis_hbm, local_ref, inverse_ref, source_ref, field_ref, faces_ref, basis_ref, sems
):
    planes, rows, cells, rank = basis_ref.shape
    slabs = slab_copies(basis_hbm, basis_ref, sems)
    for copy in slabs:
        copy.start()
    coef = total_ref[...].astype(jnp.bfloat16)
    faces = blank_faces(faces_ref)
    for x in range(planes):
        slabs[x].wait()
        slab = basis_ref[x].reshape(rows * cells, rank)
        corr = lax.dot_general(coef, slab, (((1,), (1,)), ((), ())), preferred_element_type=jnp.float32)
        corr = jnp.stack([corr[:, y * cells:(y + 1) * cells] for y in range(rows)])
        source = local_ref[x] + corr
        field = source * inverse_ref[x][:, None, :]
        put_faces(faces, field, x)
        source_ref[x] = source
        field_ref[x] = field
    for group, face in enumerate(faces):
        faces_ref[group] = face


def new_plane(refs, x, edges):
    mask_ref, field_ref, source_ref, inverse_ref, xlow_ref, xhigh_ref, ylow_ref, yhigh_ref, zlow_ref, zhigh_ref = refs
    planes, rows, chains, cells = field_ref.shape
    here = field_ref[x]
    value = source_ref[x]
    value = value + (field_ref[x + 1] if x + 1 < planes else xhigh_ref[0])
    value = value + (field_ref[x - 1] if x > 0 else xlow_ref[0])
    value = value + jnp.concatenate([here[1:], yhigh_ref[x] * mask_ref[1]], 0)
    value = value + jnp.concatenate([ylow_ref[x] * mask_ref[0], here[:-1]], 0)
    slots = cells // 2
    outer = []
    for y in range(rows):
        group, slot = divmod(x * rows + y, slots)
        outer.append(pltpu.roll(edges[group], (-2 * slot - 1) % cells, 1))
    outer = jnp.concatenate(outer, 0)
    flat = here.reshape(rows * chains, cells)
    lane = lax.broadcasted_iota(jnp.int32, flat.shape, 1)
    total = jnp.where(lane == 0, outer, pltpu.roll(flat, 1, 1))
    total = total + jnp.where(lane == cells - 1, outer, pltpu.roll(flat, cells - 1, 1))
    return (value + total.reshape(rows, chains, cells)) * inverse_ref[x][:, None, :]


def both_edges(zlow_ref, zhigh_ref):
    groups, chains, cells = zlow_ref.shape
    even = lax.broadcasted_iota(jnp.int32, (chains, cells), 1) % 2 == 0
    return [
        jnp.where(even, pltpu.roll(zhigh_ref[g], cells - 1, 1), pltpu.roll(zlow_ref[g], 1, 1))
        for g in range(groups)
    ]


def sweep_kernel(*refs):
    *inputs, out_ref, faces_ref = refs
    edges = both_edges(*inputs[-2:])
    faces = blank_faces(faces_ref)
    for x in range(out_ref.shape[0]):
        plane = new_plane(inputs, x, edges)
        out_ref[x] = plane
        put_faces(faces, plane, x)
    for group, face in enumerate(faces):
        faces_ref[group] = face


def last_kernel(*refs):
    *inputs, current_ref, out_ref = refs
    edges = both_edges(*inputs[-2:])
    for x in range(out_ref.shape[1]):
        out_ref[:, x] = current_ref[:, x] + jnp.swapaxes(new_plane(inputs, x, edges), 0, 1)


def specs(count):
    return [pl.BlockSpec(memory_space=pltpu.SMEM)] + [pl.BlockSpec(memory_space=pltpu.VMEM)] * count


def near(*arrays):
    return [pltpu.with_memory_space_constraint(a, pltpu.VMEM) for a in arrays]


def halo(field, faces):
    forward, backward = lines("gz")
    zlow = lax.ppermute(faces, "gz", forward)
    zhigh = lax.ppermute(faces, "gz", backward)
    forward, backward = lines("gx")
    xlow = lax.ppermute(field[-1:], "gx", forward)
    xhigh = lax.ppermute(field[:1], "gx", backward)
    if lax.axis_size("gy") == 2:
        send = jnp.where(lax.axis_index("gy") == 0, field[:, -1:], field[:, :1])
        ylow = yhigh = lax.ppermute(send, "gy", [(0, 1), (1, 0)])
    else:
        forward, backward = lines("gy")
        ylow = lax.ppermute(field[:, -1:], "gy", forward)
        yhigh = lax.ppermute(field[:, :1], "gy", backward)
    return xlow, xhigh, ylow, yhigh, zlow, zhigh


def body(gradient, noise_draw, current, eigvectors, eigvalues, reaction):
    chains = gradient.shape[0]
    planes, rows, cells, rank = eigvectors.shape
    last = lax.axis_size("gy") - 1
    place = lax.axis_index("gy")
    mask = jnp.where(jnp.arange(2) == 0, place > 0, place < last).astype(jnp.float32)
    total = project(gradient, noise_draw, eigvectors, eigvalues)
    for axis in ("gy", "gz", "gx"):
        total = reduce_over(total, axis)
    local = -0.5 * gradient.astype(jnp.float32) + 1.0 * noise_draw.astype(jnp.float32)
    local = jnp.transpose(local, (1, 2, 0, 3))
    inverse = 1.0 / (reaction + 6.0)
    total, local, inverse = near(total, local, inverse)

    inside = pl.BlockSpec(memory_space=pltpu.VMEM)
    limit = pltpu.CompilerParams(vmem_limit_bytes=16 * 2**20)
    whole = pltpu.VMEM((planes, rows, chains, cells), jnp.float32)
    packed = pltpu.VMEM((-(-2 * planes * rows // cells), chains, cells), jnp.float32)
    source, field, faces = pl.pallas_call(
        expand_kernel,
        in_specs=[inside, pl.BlockSpec(memory_space=pltpu.HBM), inside, inside],
        out_specs=[inside] * 3,
        out_shape=[whole, whole, packed],
        scratch_shapes=[
            pltpu.VMEM(eigvectors.shape, eigvectors.dtype),
            pltpu.SemaphoreType.DMA((planes,)),
        ],
        compiler_params=pltpu.CompilerParams(vmem_limit_bytes=56 * 2**20),
        name="expand",
    )(total, eigvectors, local, inverse)
    for _ in range(SWEEPS - 2):
        field, faces = pl.pallas_call(
            sweep_kernel,
            in_specs=specs(9),
            out_specs=[inside] * 2,
            out_shape=[whole, packed],
            compiler_params=limit,
            name="sweep",
        )(mask, *near(field, source, inverse, *halo(field, faces)))
    return pl.pallas_call(
        last_kernel,
        in_specs=specs(10),
        out_specs=inside,
        out_shape=jax.ShapeDtypeStruct(current.shape, jnp.float32),
        compiler_params=limit,
        name="last_sweep",
    )(mask, *near(field, source, inverse, *halo(field, faces), current))


def solution(mesh):
    return jax.shard_map(
        body,
        mesh=mesh,
        in_specs=(
            P(None, "gx", "gy", "gz"),
            P(None, "gx", "gy", "gz"),
            P(None, "gx", "gy", "gz"),
            P("gx", "gy", "gz", None),
            P(),
            P("gx", "gy", "gz"),
        ),
        out_specs=P(None, "gx", "gy", "gz"),
        check_vma=False,
    )
```

time: 264 us -> 84.7 us (0.32)
  the two profiles are of different devices: /device:TPU:0 before, /device:TPU:26 now
where the time goes in v2:
time: 84.7 us; the launch traced here: 84.3 us
  starting transfers between devices  33.9 us (40%)
  waiting for transfers between devices  29.3 us (35%)
  Pallas kernels  18.7 us (22%)
  other arithmetic  1.39 us (2%)
    ppermute x5, waiting for transfers between devices, reduce_over(): lax.ppermute(value, axis, [(i, i ^ step) for i in range(count)])  16.3 us
    ppermute x3, starting transfers between devices, halo(): xlow = lax.ppermute(field[-1:], 'gx', forward)  13.7 us
    ppermute x3, waiting for transfers between devices, halo(): zlow = lax.ppermute(faces, 'gz', forward)  12.6 us
    ppermute x3, starting transfers between devices, halo(): xhigh = lax.ppermute(field[:1], 'gx', backward)  6.52 us
    ppermute x3, starting transfers between devices, halo(): zhigh = lax.ppermute(faces, 'gz', backward)  6.48 us
    pallas_call x1, Pallas kernels, project(): pl.pallas_call(project_kernel, in_specs=[outside, outside, outside, insid...  6.33 us
    pallas_call x1, Pallas kernels, body(): pl.pallas_call(expand_kernel, in_specs=[inside, pl.BlockSpec(memory_space...  5.28 us
    pallas_call x2, Pallas kernels, body(): pl.pallas_call(sweep_kernel, in_specs=specs(9), out_specs=[inside] * 2, o...  4.5 us
  transfers between devices with their start and end apart: 20, of which 11 were waited for; matrix products, arithmetic and copies ran while one was open for 1% of the time, Pallas kernels for 0%

profile of v2, /device:TPU:26, one launch (start us, length us, event | category | flops | bytes accessed | tf_op | source)
XLA Modules:
  0.0 84.3 jit_solution(2805481783564154280)
XLA Ops:
  0.0 0.0 copy-start.2
  0.0 0.0 copy-start.1
  0.0 0.0 copy-start.3
  0.0 6.3 %project.1 = f32[32,512]{1,0:T(8,128)S(1)} custom-call(bf16[32,8,8,128]{3,2,1,0:T(8,128)(2,1)} %gradient_hbm.1, bf16[32,8,8,128]{3,2,1,0:T(8,128)(2,1)} %noise_hbm.1, bf16[8,8,128,512]{3,2,1,0:T(8,128)(2,1)} %basis_hbm.3, f32[1,512]{1,0:T(1,128)} %bitcast.3), custom_call_target="tpu_custom_call" | custom-call | tf_op jit(solution)/shard_map/project/pallas_call | solution.py:84
  6.3 0.1 collective-permute-start
  6.4 1.2 %collective-permute-done = f32[32,512]{1,0:T(8,128)S(1)} collective-permute-done((f32[32,512]{1,0:T(8,128)S(1)}, f32[32,512]{1,0:T(8,128)S(1)}, u32[]{:S(2)}, u32[]{:S(2)}) %collective-permute-start) | collective-permute-done | bytes 65568 | tf_op jit(solution)/shard_map/ppermute | solution.py:17
  7.7 0.5 collective-permute-start.1
  8.2 3.8 %collective-permute-done.1 = f32[32,512]{1,0:T(8,128)S(1)} collective-permute-done((f32[32,512]{1,0:T(8,128)S(1)}, f32[32,512]{1,0:T(8,128)S(1)}, u32[]{:S(2)}, u32[]{:S(2)}) %collective-permute-start.1) | collective-permute-done | bytes 65568 | tf_op jit(solution)/shard_map/ppermute | solution.py:17
  12.0 0.4 collective-permute-start.2
  12.4 5.4 %collective-permute-done.2 = f32[32,512]{1,0:T(8,128)S(1)} collective-permute-done((f32[32,512]{1,0:T(8,128)S(1)}, f32[32,512]{1,0:T(8,128)S(1)}, u32[]{:S(2)}, u32[]{:S(2)}) %collective-permute-start.2) | collective-permute-done | bytes 65568 | tf_op jit(solution)/shard_map/ppermute | solution.py:17
  17.9 0.6 collective-permute-start.3
  18.5 0.0 copy-done.2
  18.5 0.0 copy-done.1
  18.5 0.6 add_bitcast_fusion.local_ref
  19.1 3.1 %collective-permute-done.3 = f32[32,512]{1,0:T(8,128)S(1)} collective-permute-done((f32[32,512]{1,0:T(8,128)S(1)}, f32[32,512]{1,0:T(8,128)S(1)}, u32[]{:S(2)}, u32[]{:S(2)}) %collective-permute-start.3) | collective-permute-done | bytes 65568 | tf_op jit(solution)/shard_map/ppermute | solution.py:17
  22.2 1.6 %collective-permute-start.4 = (f32[32,512]{1,0:T(8,128)S(1)}, f32[32,512]{1,0:T(8,128)S(1)}, u32[]{:S(2)}, u32[]{:S(2)}) collective-permute-start(f32[32,512]{1,0:T(8,128)S(1)} %add.27), channel_id=1, source_target_pairs={{0,16},{8,24},{16,0},{24,8},{1,17},{9,25},{17,1},{25,9},{2,18},{10... | collective-permute-start | bytes 196616 | tf_op jit(solution)/shard_map/ppermute | solution.py:17
  23.8 0.0 copy-done.3
  23.8 2.7 %collective-permute-done.4 = f32[32,512]{1,0:T(8,128)S(1)} collective-permute-done((f32[32,512]{1,0:T(8,128)S(1)}, f32[32,512]{1,0:T(8,128)S(1)}, u32[]{:S(2)}, u32[]{:S(2)}) %collective-permute-start.4) | collective-permute-done | bytes 65568 | tf_op jit(solution)/shard_map/ppermute | solution.py:17
  26.5 5.3 %expand.1 = (f32[8,8,32,128]{3,2,1,0:T(8,128)S(1)}, f32[8,8,32,128]{3,2,1,0:T(8,128)S(1)}, f32[1,32,128]{2,1,0:T(8,128)S(1)}) custom-call(f32[32,512]{1,0:T(8,128)S(1)} %add.28.total_ref, bf16[8,8,128,512]{3,2,1,0:T(8,128)(2,1)} %basis_hbm.3, f32[8,8,32,128]{3,2,1,0:T(8,128)S(1)} %add_bitcast_fusion.local_ref, ...), custom_call_target="tpu_custom_call" | custom-call | tf_op jit(solution)/shard_map/expand/pallas_call | solution.py:217
  31.8 0.0 copy-start
  31.8 0.7 fusion.2
  32.6 0.7 slice_select_fusion.2
  33.2 0.0 collective-permute-start.7
  33.2 2.4 %collective-permute-start.6 = (f32[1,8,32,128]{3,2,1,0:T(8,128)}, f32[1,8,32,128]{3,2,1,0:T(8,128)S(1)}, u32[]{:S(2)}, u32[]{:S(2)}) collective-permute-start(f32[1,8,32,128]{3,2,1,0:T(8,128)} %get-tuple-element.23), channel_id=1, source_target_pairs={{8,0},{16,8},{24,16},{9,1},{17,9},{25,17},{10,2},{18,10},{26,18},{... | collective-permute-start | bytes 393224 | tf_op jit(solution)/shard_map/ppermute | solution.py:188
  35.7 4.3 %collective-permute-start.5 = (f32[1,8,32,128]{3,2,1,0:T(8,128)}, f32[1,8,32,128]{3,2,1,0:T(8,128)}, u32[]{:S(2)}, u32[]{:S(2)}) collective-permute-start(f32[1,8,32,128]{3,2,1,0:T(8,128)} %get-tuple-element.24), channel_id=1, source_target_pairs={{0,8},{8,16},{16,24},{1,9},{9,17},{17,25},{2,10},{10,18},{18,26},{... | collective-permute-start | bytes 393224 | tf_op jit(solution)/shard_map/ppermute | solution.py:187
  40.0 1.8 %collective-permute-start.9 = (f32[1,32,128]{2,1,0:T(8,128)S(1)}, f32[1,32,128]{2,1,0:T(8,128)S(1)}, u32[]{:S(2)}, u32[]{:S(2)}) collective-permute-start(f32[1,32,128]{2,1,0:T(8,128)S(1)} %get-tuple-element.14), channel_id=1, source_target_pairs={{1,0},{2,1},{3,2},{5,4},{6,5},{7,6},{9,8},{10,9},{11,10},{13,12},{... | collective-permute-start | bytes 49160 | tf_op jit(solution)/shard_map/ppermute | solution.py:185
  41.8 1.3 %collective-permute-start.8 = (f32[1,32,128]{2,1,0:T(8,128)S(1)}, f32[1,32,128]{2,1,0:T(8,128)S(1)}, u32[]{:S(2)}, u32[]{:S(2)}) collective-permute-start(f32[1,32,128]{2,1,0:T(8,128)S(1)} %get-tuple-element.14), channel_id=1, source_target_pairs={{0,1},{1,2},{2,3},{4,5},{5,6},{6,7},{8,9},{9,10},{10,11},{12,13},{... | collective-permute-start | bytes 49160 | tf_op jit(solution)/shard_map/ppermute | solution.py:184
  43.1 0.1 collective-permute-done.9.refs_9_
  43.2 4.2 %collective-permute-done.8.refs_8_ = f32[1,32,128]{2,1,0:T(8,128)S(1)} collective-permute-done((f32[1,32,128]{2,1,0:T(8,128)S(1)}, f32[1,32,128]{2,1,0:T(8,128)S(1)}, u32[]{:S(2)}, u32[]{:S(2)}) %collective-permute-start.8) | collective-permute-done | bytes 16416 | tf_op jit(solution)/shard_map/ppermute | solution.py:184
  47.4 0.0 collective-permute-done.7.refs_6_.refs_7_
  47.4 0.0 collective-permute-done.6.refs_5_
  47.4 0.0 collective-permute-done.5.refs_4_
  47.5 2.4 %sweep.2 = (f32[8,8,32,128]{3,2,1,0:T(8,128)S(1)}, f32[1,32,128]{2,1,0:T(8,128)S(1)}) custom-call(f32[2]{0:T(128)S(1)} %select_convert_fusion.refs_0_, f32[8,8,32,128]{3,2,1,0:T(8,128)S(1)} %get-tuple-element.12.refs_1_, f32[8,8,32,128]{3,2,1,0:T(8,128)S(1)} %get-tuple-element.13.refs_2_, f32[8,8,128]{2,1,0:T(8,128)S(1)} %add_divide_fusion.inverse_ref.refs_3_, ...), custom_call_target="tpu_custom_call" | custom-call | tf_op jit(solution)/shard_map/sweep/pallas_call | solution.py:230
  49.9 0.1 collective-permute-start.12
  50.0 2.2 %collective-permute-start.11 = (f32[1,8,32,128]{3,2,1,0:T(8,128)S(1)}, f32[1,8,32,128]{3,2,1,0:T(8,128)S(1)}, u32[]{:S(2)}, u32[]{:S(2)}) collective-permute-start(f32[1,8,32,128]{3,2,1,0:T(8,128)S(1)} %get-tuple-element.21), channel_id=1, source_target_pairs={{8,0},{16,8},{24,16},{9,1},{17,9},{25,17},{10,2},{18,10},{26,18},{... | collective-permute-start | bytes 393224 | tf_op jit(solution)/shard_map/ppermute | solution.py:188
  52.2 4.6 %collective-permute-start.10 = (f32[1,8,32,128]{3,2,1,0:T(8,128)S(1)}, f32[1,8,32,128]{3,2,1,0:T(8,128)S(1)}, u32[]{:S(2)}, u32[]{:S(2)}) collective-permute-start(f32[1,8,32,128]{3,2,1,0:T(8,128)S(1)} %get-tuple-element.22), channel_id=1, source_target_pairs={{0,8},{8,16},{16,24},{1,9},{9,17},{17,25},{2,10},{10,18},{18,26},{... | collective-permute-start | bytes 393224 | tf_op jit(solution)/shard_map/ppermute | solution.py:187
  56.8 2.3 %collective-permute-start.14 = (f32[1,32,128]{2,1,0:T(8,128)S(1)}, f32[1,32,128]{2,1,0:T(8,128)S(1)}, u32[]{:S(2)}, u32[]{:S(2)}) collective-permute-start(f32[1,32,128]{2,1,0:T(8,128)S(1)} %get-tuple-element.16), channel_id=1, source_target_pairs={{1,0},{2,1},{3,2},{5,4},{6,5},{7,6},{9,8},{10,9},{11,10},{13,12},{... | collective-permute-start | bytes 49160 | tf_op jit(solution)/shard_map/ppermute | solution.py:185
  59.1 1.3 %collective-permute-start.13 = (f32[1,32,128]{2,1,0:T(8,128)S(1)}, f32[1,32,128]{2,1,0:T(8,128)S(1)}, u32[]{:S(2)}, u32[]{:S(2)}) collective-permute-start(f32[1,32,128]{2,1,0:T(8,128)S(1)} %get-tuple-element.16), channel_id=1, source_target_pairs={{0,1},{1,2},{2,3},{4,5},{5,6},{6,7},{8,9},{9,10},{10,11},{12,13},{... | collective-permute-start | bytes 49160 | tf_op jit(solution)/shard_map/ppermute | solution.py:184
  60.4 0.1 collective-permute-done.14.refs_9_
  60.5 4.2 %collective-permute-done.13.refs_8_ = f32[1,32,128]{2,1,0:T(8,128)S(1)} collective-permute-done((f32[1,32,128]{2,1,0:T(8,128)S(1)}, f32[1,32,128]{2,1,0:T(8,128)S(1)}, u32[]{:S(2)}, u32[]{:S(2)}) %collective-permute-start.13) | collective-permute-done | bytes 16416 | tf_op jit(solution)/shard_map/ppermute | solution.py:184
  64.7 0.0 collective-permute-done.12.refs_6_.refs_7_
  64.7 0.0 collective-permute-done.11.refs_5_
  64.7 0.0 collective-permute-done.10.refs_4_
  64.7 2.1 %sweep.3 = (f32[8,8,32,128]{3,2,1,0:T(8,128)S(1)}, f32[1,32,128]{2,1,0:T(8,128)S(1)}) custom-call(f32[2]{0:T(128)S(1)} %select_convert_fusion.refs_0_, f32[8,8,32,128]{3,2,1,0:T(8,128)S(1)} %get-tuple-element.15.refs_1_, f32[8,8,32,128]{3,2,1,0:T(8,128)S(1)} %get-tuple-element.13.refs_2_, f32[8,8,128]{2,1,0:T(8,128)S(1)} %add_divide_fusion.inverse_ref.refs_3_, ...), custom_call_target="tpu_custom_call" | custom-call | tf_op jit(solution)/shard_map/sweep/pallas_call | solution.py:230
  66.8 0.1 collective-permute-start.17
  66.9 1.9 %collective-permute-start.16 = (f32[1,8,32,128]{3,2,1,0:T(8,128)S(1)}, f32[1,8,32,128]{3,2,1,0:T(8,128)S(1)}, u32[]{:S(2)}, u32[]{:S(2)}) collective-permute-start(f32[1,8,32,128]{3,2,1,0:T(8,128)S(1)} %get-tuple-element.19), channel_id=1, source_target_pairs={{8,0},{16,8},{24,16},{9,1},{17,9},{25,17},{10,2},{18,10},{26,18},{... | collective-permute-start | bytes 393224 | tf_op jit(solution)/shard_map/ppermute | solution.py:188
  68.9 4.8 %collective-permute-start.15 = (f32[1,8,32,128]{3,2,1,0:T(8,128)S(1)}, f32[1,8,32,128]{3,2,1,0:T(8,128)S(1)}, u32[]{:S(2)}, u32[]{:S(2)}) collective-permute-start(f32[1,8,32,128]{3,2,1,0:T(8,128)S(1)} %get-tuple-element.20), channel_id=1, source_target_pairs={{0,8},{8,16},{16,24},{1,9},{9,17},{17,25},{2,10},{10,18},{18,26},{... | collective-permute-start | bytes 393224 | tf_op jit(solution)/shard_map/ppermute | solution.py:187
  73.7 2.4 %collective-permute-start.19 = (f32[1,32,128]{2,1,0:T(8,128)S(1)}, f32[1,32,128]{2,1,0:T(8,128)S(1)}, u32[]{:S(2)}, u32[]{:S(2)}) collective-permute-start(f32[1,32,128]{2,1,0:T(8,128)S(1)} %get-tuple-element.18), channel_id=1, source_target_pairs={{1,0},{2,1},{3,2},{5,4},{6,5},{7,6},{9,8},{10,9},{11,10},{13,12},{... | collective-permute-start | bytes 49160 | tf_op jit(solution)/shard_map/ppermute | solution.py:185
  76.0 1.3 %collective-permute-start.18 = (f32[1,32,128]{2,1,0:T(8,128)S(1)}, f32[1,32,128]{2,1,0:T(8,128)S(1)}, u32[]{:S(2)}, u32[]{:S(2)}) collective-permute-start(f32[1,32,128]{2,1,0:T(8,128)S(1)} %get-tuple-element.18), channel_id=1, source_target_pairs={{0,1},{1,2},{2,3},{4,5},{5,6},{6,7},{8,9},{9,10},{10,11},{12,13},{... | collective-permute-start | bytes 49160 | tf_op jit(solution)/shard_map/ppermute | solution.py:184
  77.3 0.1 collective-permute-done.19.refs_9_
  77.5 4.2 %collective-permute-done.18.refs_8_ = f32[1,32,128]{2,1,0:T(8,128)S(1)} collective-permute-done((f32[1,32,128]{2,1,0:T(8,128)S(1)}, f32[1,32,128]{2,1,0:T(8,128)S(1)}, u32[]{:S(2)}, u32[]{:S(2)}) %collective-permute-start.18) | collective-permute-done | bytes 16416 | tf_op jit(solution)/shard_map/ppermute | solution.py:184
  81.7 0.0 collective-permute-done.17.refs_6_.refs_7_
  81.7 0.0 collective-permute-done.16.refs_5_
  81.7 0.0 collective-permute-done.15.refs_4_
  81.7 0.0 copy-done
  81.7 2.6 %last_sweep.1 = f32[32,8,8,128]{3,2,1,0:T(8,128)} custom-call(f32[2]{0:T(128)S(1)} %select_convert_fusion.refs_0_, f32[8,8,32,128]{3,2,1,0:T(8,128)S(1)} %get-tuple-element.17.refs_1_, f32[8,8,32,128]{3,2,1,0:T(8,128)S(1)} %get-tuple-element.13.refs_2_, f32[8,8,128]{2,1,0:T(8,128)S(1)} %add_divide_fusion.inverse_ref.refs_3_, ...), custom_call_target="tpu_custom_call" | custom-call | tf_op jit(solution)/shard_map/last_sweep/pallas_call | solution.py:238
  (11 shorter events, 0.1 us)
Async XLA Ops:
  0.0 18.5 %copy-start.2 = (bf16[32,8,8,128]{3,2,1,0:T(8,128)(2,1)S(1)}, bf16[32,8,8,128]{3,2,1,0:T(8,128)(2,1)}, u32[]{:S(2)}) copy-start(bf16[32,8,8,128]{3,2,1,0:T(8,128)(2,1)} %noise_hbm.1) | copy-start | bytes 1572868
  0.0 18.5 %copy-start.1 = (bf16[32,8,8,128]{3,2,1,0:T(8,128)(2,1)S(1)}, bf16[32,8,8,128]{3,2,1,0:T(8,128)(2,1)}, u32[]{:S(2)}) copy-start(bf16[32,8,8,128]{3,2,1,0:T(8,128)(2,1)} %gradient_hbm.1) | copy-start | bytes 1572868
  0.0 23.8 %copy-start.3 = (f32[8,8,128]{2,1,0:T(8,128)S(1)}, f32[8,8,128]{2,1,0:T(8,128)}, u32[]{:S(2)}) copy-start(f32[8,8,128]{2,1,0:T(8,128)} %param.11) | copy-start | bytes 98308
  6.3 1.3 %collective-permute-start = (f32[32,512]{1,0:T(8,128)S(1)}, f32[32,512]{1,0:T(8,128)S(1)}, u32[]{:S(2)}, u32[]{:S(2)}) collective-permute-start(f32[32,512]{1,0:T(8,128)S(1)} %project.1), channel_id=1, source_target_pairs={{0,4},{4,0},{1,5},{5,1},{2,6},{6,2},{3,7},{7,3},{8,12},{12,8},{9,1... | collective-permute-start | bytes 196616 | tf_op jit(solution)/shard_map/ppermute | solution.py:17
  7.7 4.3 %collective-permute-start.1 = (f32[32,512]{1,0:T(8,128)S(1)}, f32[32,512]{1,0:T(8,128)S(1)}, u32[]{:S(2)}, u32[]{:S(2)}) collective-permute-start(f32[32,512]{1,0:T(8,128)S(1)} %add.24), channel_id=1, source_target_pairs={{0,1},{1,0},{2,3},{3,2},{4,5},{5,4},{6,7},{7,6},{8,9},{9,8},{10,11... | collective-permute-start | bytes 196616 | tf_op jit(solution)/shard_map/ppermute | solution.py:17
  12.0 5.8 %collective-permute-start.2 = (f32[32,512]{1,0:T(8,128)S(1)}, f32[32,512]{1,0:T(8,128)S(1)}, u32[]{:S(2)}, u32[]{:S(2)}) collective-permute-start(f32[32,512]{1,0:T(8,128)S(1)} %add.25), channel_id=1, source_target_pairs={{0,2},{1,3},{2,0},{3,1},{4,6},{5,7},{6,4},{7,5},{8,10},{9,11},{10,... | collective-permute-start | bytes 196616 | tf_op jit(solution)/shard_map/ppermute | solution.py:17
  17.9 4.3 %collective-permute-start.3 = (f32[32,512]{1,0:T(8,128)S(1)}, f32[32,512]{1,0:T(8,128)S(1)}, u32[]{:S(2)}, u32[]{:S(2)}) collective-permute-start(f32[32,512]{1,0:T(8,128)S(1)} %add.26), channel_id=1, source_target_pairs={{0,8},{8,0},{16,24},{24,16},{1,9},{9,1},{17,25},{25,17},{2,10},{10... | collective-permute-start | bytes 196616 | tf_op jit(solution)/shard_map/ppermute | solution.py:17
  22.2 4.3 %collective-permute-start.4 = (f32[32,512]{1,0:T(8,128)S(1)}, f32[32,512]{1,0:T(8,128)S(1)}, u32[]{:S(2)}, u32[]{:S(2)}) collective-permute-start(f32[32,512]{1,0:T(8,128)S(1)} %add.27), channel_id=1, source_target_pairs={{0,16},{8,24},{16,0},{24,8},{1,17},{9,25},{17,1},{25,9},{2,18},{10... | collective-permute-start | bytes 196616 | tf_op jit(solution)/shard_map/ppermute | solution.py:17
  31.8 49.9 %copy-start = (f32[32,8,8,128]{3,2,1,0:T(8,128)S(1)}, f32[32,8,8,128]{3,2,1,0:T(8,128)}, u32[]{:S(2)}) copy-start(f32[32,8,8,128]{3,2,1,0:T(8,128)} %refs_10_.1) | copy-start | bytes 3145732
  33.2 14.2 %collective-permute-start.7 = (f32[8,1,32,128]{3,2,1,0:T(8,128)}, f32[8,1,32,128]{3,2,1,0:T(8,128)S(1)}, u32[]{:S(2)}, u32[]{:S(2)}) collective-permute-start(f32[8,1,32,128]{3,2,1,0:T(8,128)} %slice_select_fusion.2), channel_id=1, source_target_pairs={{0,4},{4,0},{1,5},{5,1},{2,6},{6,2},{3,7},{7,3},{8,12},{12,8},{9,1... | collective-permute-start | bytes 393224 | tf_op jit(solution)/shard_map/ppermute | solution.py:191
  33.2 14.2 %collective-permute-start.6 = (f32[1,8,32,128]{3,2,1,0:T(8,128)}, f32[1,8,32,128]{3,2,1,0:T(8,128)S(1)}, u32[]{:S(2)}, u32[]{:S(2)}) collective-permute-start(f32[1,8,32,128]{3,2,1,0:T(8,128)} %get-tuple-element.23), channel_id=1, source_target_pairs={{8,0},{16,8},{24,16},{9,1},{17,9},{25,17},{10,2},{18,10},{26,18},{... | collective-permute-start | bytes 393224 | tf_op jit(solution)/shard_map/ppermute | solution.py:188
  35.7 11.8 %collective-permute-start.5 = (f32[1,8,32,128]{3,2,1,0:T(8,128)}, f32[1,8,32,128]{3,2,1,0:T(8,128)}, u32[]{:S(2)}, u32[]{:S(2)}) collective-permute-start(f32[1,8,32,128]{3,2,1,0:T(8,128)} %get-tuple-element.24), channel_id=1, source_target_pairs={{0,8},{8,16},{16,24},{1,9},{9,17},{17,25},{2,10},{10,18},{18,26},{... | collective-permute-start | bytes 393224 | tf_op jit(solution)/shard_map/ppermute | solution.py:187
  40.0 3.3 %collective-permute-start.9 = (f32[1,32,128]{2,1,0:T(8,128)S(1)}, f32[1,32,128]{2,1,0:T(8,128)S(1)}, u32[]{:S(2)}, u32[]{:S(2)}) collective-permute-start(f32[1,32,128]{2,1,0:T(8,128)S(1)} %get-tuple-element.14), channel_id=1, source_target_pairs={{1,0},{2,1},{3,2},{5,4},{6,5},{7,6},{9,8},{10,9},{11,10},{13,12},{... | collective-permute-start | bytes 49160 | tf_op jit(solution)/shard_map/ppermute | solution.py:185
  41.8 5.6 %collective-permute-start.8 = (f32[1,32,128]{2,1,0:T(8,128)S(1)}, f32[1,32,128]{2,1,0:T(8,128)S(1)}, u32[]{:S(2)}, u32[]{:S(2)}) collective-permute-start(f32[1,32,128]{2,1,0:T(8,128)S(1)} %get-tuple-element.14), channel_id=1, source_target_pairs={{0,1},{1,2},{2,3},{4,5},{5,6},{6,7},{8,9},{9,10},{10,11},{12,13},{... | collective-permute-start | bytes 49160 | tf_op jit(solution)/shard_map/ppermute | solution.py:184
  49.9 14.8 %collective-permute-start.12 = (f32[8,1,32,128]{3,2,1,0:T(8,128)S(1)}, f32[8,1,32,128]{3,2,1,0:T(8,128)S(1)}, u32[]{:S(2)}, u32[]{:S(2)}) collective-permute-start(f32[8,1,32,128]{3,2,1,0:T(8,128)S(1)} %slice_select_fusion.1), channel_id=1, source_target_pairs={{0,4},{4,0},{1,5},{5,1},{2,6},{6,2},{3,7},{7,3},{8,12},{12,8},{9,1... | collective-permute-start | bytes 393224 | tf_op jit(solution)/shard_map/ppermute | solution.py:191
  50.0 14.7 %collective-permute-start.11 = (f32[1,8,32,128]{3,2,1,0:T(8,128)S(1)}, f32[1,8,32,128]{3,2,1,0:T(8,128)S(1)}, u32[]{:S(2)}, u32[]{:S(2)}) collective-permute-start(f32[1,8,32,128]{3,2,1,0:T(8,128)S(1)} %get-tuple-element.21), channel_id=1, source_target_pairs={{8,0},{16,8},{24,16},{9,1},{17,9},{25,17},{10,2},{18,10},{26,18},{... | collective-permute-start | bytes 393224 | tf_op jit(solution)/shard_map/ppermute | solution.py:188
  52.2 12.5 %collective-permute-start.10 = (f32[1,8,32,128]{3,2,1,0:T(8,128)S(1)}, f32[1,8,32,128]{3,2,1,0:T(8,128)S(1)}, u32[]{:S(2)}, u32[]{:S(2)}) collective-permute-start(f32[1,8,32,128]{3,2,1,0:T(8,128)S(1)} %get-tuple-element.22), channel_id=1, source_target_pairs={{0,8},{8,16},{16,24},{1,9},{9,17},{17,25},{2,10},{10,18},{18,26},{... | collective-permute-start | bytes 393224 | tf_op jit(solution)/shard_map/ppermute | solution.py:187
  56.8 3.7 %collective-permute-start.14 = (f32[1,32,128]{2,1,0:T(8,128)S(1)}, f32[1,32,128]{2,1,0:T(8,128)S(1)}, u32[]{:S(2)}, u32[]{:S(2)}) collective-permute-start(f32[1,32,128]{2,1,0:T(8,128)S(1)} %get-tuple-element.16), channel_id=1, source_target_pairs={{1,0},{2,1},{3,2},{5,4},{6,5},{7,6},{9,8},{10,9},{11,10},{13,12},{... | collective-permute-start | bytes 49160 | tf_op jit(solution)/shard_map/ppermute | solution.py:185
  59.1 5.6 %collective-permute-start.13 = (f32[1,32,128]{2,1,0:T(8,128)S(1)}, f32[1,32,128]{2,1,0:T(8,128)S(1)}, u32[]{:S(2)}, u32[]{:S(2)}) collective-permute-start(f32[1,32,128]{2,1,0:T(8,128)S(1)} %get-tuple-element.16), channel_id=1, source_target_pairs={{0,1},{1,2},{2,3},{4,5},{5,6},{6,7},{8,9},{9,10},{10,11},{12,13},{... | collective-permute-start | bytes 49160 | tf_op jit(solution)/shard_map/ppermute | solution.py:184
  66.8 14.8 %collective-permute-start.17 = (f32[8,1,32,128]{3,2,1,0:T(8,128)S(1)}, f32[8,1,32,128]{3,2,1,0:T(8,128)S(1)}, u32[]{:S(2)}, u32[]{:S(2)}) collective-permute-start(f32[8,1,32,128]{3,2,1,0:T(8,128)S(1)} %slice_select_fusion), channel_id=1, source_target_pairs={{0,4},{4,0},{1,5},{5,1},{2,6},{6,2},{3,7},{7,3},{8,12},{12,8},{9,1... | collective-permute-start | bytes 393224 | tf_op jit(solution)/shard_map/ppermute | solution.py:191
  66.9 14.8 %collective-permute-start.16 = (f32[1,8,32,128]{3,2,1,0:T(8,128)S(1)}, f32[1,8,32,128]{3,2,1,0:T(8,128)S(1)}, u32[]{:S(2)}, u32[]{:S(2)}) collective-permute-start(f32[1,8,32,128]{3,2,1,0:T(8,128)S(1)} %get-tuple-element.19), channel_id=1, source_target_pairs={{8,0},{16,8},{24,16},{9,1},{17,9},{25,17},{10,2},{18,10},{26,18},{... | collective-permute-start | bytes 393224 | tf_op jit(solution)/shard_map/ppermute | solution.py:188
  68.9 12.8 %collective-permute-start.15 = (f32[1,8,32,128]{3,2,1,0:T(8,128)S(1)}, f32[1,8,32,128]{3,2,1,0:T(8,128)S(1)}, u32[]{:S(2)}, u32[]{:S(2)}) collective-permute-start(f32[1,8,32,128]{3,2,1,0:T(8,128)S(1)} %get-tuple-element.20), channel_id=1, source_target_pairs={{0,8},{8,16},{16,24},{1,9},{9,17},{17,25},{2,10},{10,18},{18,26},{... | collective-permute-start | bytes 393224 | tf_op jit(solution)/shard_map/ppermute | solution.py:187
  73.7 3.8 %collective-permute-start.19 = (f32[1,32,128]{2,1,0:T(8,128)S(1)}, f32[1,32,128]{2,1,0:T(8,128)S(1)}, u32[]{:S(2)}, u32[]{:S(2)}) collective-permute-start(f32[1,32,128]{2,1,0:T(8,128)S(1)} %get-tuple-element.18), channel_id=1, source_target_pairs={{1,0},{2,1},{3,2},{5,4},{6,5},{7,6},{9,8},{10,9},{11,10},{13,12},{... | collective-permute-start | bytes 49160 | tf_op jit(solution)/shard_map/ppermute | solution.py:185
  76.0 5.6 %collective-permute-start.18 = (f32[1,32,128]{2,1,0:T(8,128)S(1)}, f32[1,32,128]{2,1,0:T(8,128)S(1)}, u32[]{:S(2)}, u32[]{:S(2)}) collective-permute-start(f32[1,32,128]{2,1,0:T(8,128)S(1)} %get-tuple-element.18), channel_id=1, source_target_pairs={{0,1},{1,2},{2,3},{4,5},{5,6},{6,7},{8,9},{9,10},{10,11},{12,13},{... | collective-permute-start | bytes 49160 | tf_op jit(solution)/shard_map/ppermute | solution.py:184
